TPU v7x, 256 devices: a whole 4x4x8 slice. The times are simulated.
256 devices in a mesh: grp: 8 (over z), dev: 32 (over y, x, core).
Axes of the slice: x: 4, y: 4, z: 8, core: 2. Of those that a mesh axis runs over, the one named last changes fastest.
Arguments:
- layer_inputs: bfloat16 [8, 8192, 4096], P(None, 'grp', 'dev')
- output_grads: bfloat16 [8, 8192, 2048], P(None, ('grp', 'dev'))
- layer_owner: int32 [8], replicated, may hold values from 0 to 7, each once
- master_weights: float32 [8, 4096, 2048], P('grp', 'dev')
- momentum: float32 [8, 4096, 2048], P('grp', 'dev'), may hold values from -6 to 6
- table_blocks: float32 [8, 256, 128, 128], P('grp', 'dev'), may hold values from -6 to 6
- block_grads: bfloat16 [8, 32, 64, 128, 128], P('grp', 'dev'), may hold values from -6 to 6
- block_ids: int32 [8, 32, 64], P('grp', 'dev'), may hold values from 0 to 7
- block_counts: int32 [8, 32, 32], P('grp', 'dev'), may hold values from 0 to 2, as said below
Outputs:
- new_master: float32 [8, 4096, 2048], P('grp', 'dev')
- new_momentum: float32 [8, 4096, 2048], P('grp', 'dev')
- new_weights: bfloat16 [8, 4096, 2048], P(None, 'dev')
- new_table: float32 [8, 256, 128, 128], P('grp', 'dev')
Inputs may be any that keep to these rules, and one draw needn't show every extreme that they name: `layer_owner`: each group owns exactly one layer. `block_ids`: several live slots may name the same block; their gradients add. `block_counts`: in every group some owners receive 2 live slots from every device; slots at or past the count hold stale data.
All inputs are finite; a program needn't handle non-finite values.
Results may differ from a plain program's by a relative error of at most 0.001.
Values may be sent and summed in bfloat16 or wider, within the bound.
A program may use at most 128 MiB of HBM per device.

v0:
```python
import functools

import jax
import jax.numpy as jnp
from jax import lax
from jax.experimental import pallas as pl
from jax.experimental.pallas import tpu as pltpu
from jax.sharding import PartitionSpec as P

tower_rate = 0.5
momentum_keep = 0.9
tower_decay = 0.1
table_rate = 0.5
table_decay = 0.2
eps_norm = 1e-06

NZ = 8
NX = 4
NY = 4
ND = NX * NY * 2
NCHIP = NX * NY


def step_kernel(
    owner,
    ids,
    counts,
    x_hbm,
    g_hbm,
    w_hbm,
    m_hbm,
    t_hbm,
    bg_hbm,
    slots_out,
    w_out,
    m_out,
    t_out,
    x_in,
    x_slot,
    x_all,
    x_turn,
    g_in,
    g_slot,
    g_all,
    acc,
    grad,
    w,
    m,
    table,
    sums,
    got,
    tag,
    got_tag,
    norms,
    slabs,
    in_sem,
    out_sem,
    gz_send,
    gz_recv,
    xz_send,
    xz_recv,
    xp_send,
    xp_recv,
    ag_send,
    r1,
    r2,
    r3,
    r4,
    half_send,
    half_recv,
    norm_send,
    norm_recv,
    bg_send,
    bg_recv,
    tag_send,
    tag_recv,
    own_sem,
    wz_send,
    wz_recv,
    slab_sem,
):
    z = lax.axis_index("grp")
    d = lax.axis_index("dev")
    core = d % 2
    cx = (d // 2) % NX
    cy = d // (2 * NX)
    chip = d // 2
    pal = chip * 2 + 1 - core
    rows = w_hbm.shape[1]
    cols = w_hbm.shape[2]
    half = cols // 2
    per = g_hbm.shape[1]
    pair = 2 * per
    tokens = x_hbm.shape[1]

    def spot(a, b):
        sx = (cx + a * (1 - core) + b * core + NX) % NX
        sy = (cy + a * core + b * (1 - core) + NY) % NY
        return sy * NX + sx

    def send(src, dst, s_sem, r_sem, zz, dd):
        pltpu.make_async_remote_copy(
            src_ref=src,
            dst_ref=dst,
            send_sem=s_sem,
            recv_sem=r_sem,
            device_id=(zz, dd),
            device_id_type=pl.DeviceIdType.MESH,
        ).start()

    def arrived(ref, sem):
        pltpu.make_async_copy(ref, ref, sem).wait()

    def column(i):
        off = (i % 2) * ((i + 1) // 2) + (1 - i % 2) * (NZ - i // 2)
        return (z + off) % NZ

    x_load = pltpu.make_async_copy(x_hbm, x_in, in_sem.at[0])
    g_load = pltpu.make_async_copy(g_hbm, g_in, in_sem.at[1])
    g_load.start()
    x_load.start()
    w_load = pltpu.make_async_copy(w_hbm.at[0], w, in_sem.at[2])
    m_load = pltpu.make_async_copy(m_hbm.at[0], m, in_sem.at[3])
    t_load = pltpu.make_async_copy(t_hbm.at[0], table, in_sem.at[4])
    own_load = pltpu.make_async_copy(
        bg_hbm.at[0, 0, pl.ds(2 * d, 2)], got.at[pl.ds(2 * d, 2)], own_sem
    )
    w_load.start()
    m_load.start()
    t_load.start()
    own_load.start()

    barrier = pltpu.get_barrier_semaphore()

    @pl.loop(1, ND)
    def _(p):
        pl.semaphore_signal(
            barrier, inc=1, device_id=(z, (d + p) % ND), device_id_type=pl.DeviceIdType.MESH
        )

    @pl.loop(1, NZ)
    def _(p):
        for cc in range(2):
            pl.semaphore_signal(
                barrier,
                inc=1,
                device_id=((z + p) % NZ, chip * 2 + cc),
                device_id_type=pl.DeviceIdType.MESH,
            )

    def layer_of(s):
        found = jnp.int32(0)
        for l in range(NZ):
            found = jnp.where(owner[l] == s, l, found)
        return found

    g_load.wait()

    @pl.loop(0, NZ)
    def _(s):
        l = layer_of(s)
        for h in range(2):
            g_slot[h, s] = g_in[l, :, h * half : (h + 1) * half]

    g_all[z, chip, pl.ds(core * per, per), :] = g_slot[core, z]
    x_load.wait()

    @pl.loop(0, NZ)
    def _(s):
        l = layer_of(s)
        x_slot[s] = x_in[l]

    x_all[z, core] = x_slot[z]

    pl.semaphore_wait(barrier, ND - 1 + 2 * (NZ - 1))

    send(
        g_slot.at[1 - core, z],
        g_all.at[z, chip, pl.ds(core * per, per)],
        gz_send.at[1],
        gz_recv.at[z, core],
        z,
        pal,
    )

    @pl.loop(1, NZ)
    def _(i):
        zt = column(i)
        for cc in range(2):
            send(
                g_slot.at[cc, zt],
                g_all.at[z, chip, pl.ds(core * per, per)],
                gz_send.at[0],
                gz_recv.at[z, core],
                zt,
                chip * 2 + cc,
            )

    send(x_all.at[z, core], x_all.at[z, core], xp_send, xp_recv.at[z], z, pal)

    @pl.loop(1, NZ)
    def _(i):
        zt = column(i)
        send(x_slot.at[zt], x_all.at[z, core], xz_send, xz_recv.at[z], zt, d)

    @pl.loop(0, ND)
    def _(j):
        for r in range(2):
            t = jnp.where(r < counts[0, 0, j], ids[0, 0, 2 * j + r], -1)
            tag[j, r : r + 1, :] = jnp.full((1, tag.shape[2]), t, jnp.int32)

    got_tag[d] = tag[d]
    acc[...] = jnp.zeros_like(acc)
    w_load.wait()
    weight_sq = jnp.zeros((8, 128), jnp.float32)

    def weight_step(i, total):
        v = w[pl.ds(pl.multiple_of(i * 8, 8), 8), :]
        v = v * v
        for k in range(cols // 128):
            total = total + v[:, k * 128 : (k + 1) * 128]
        return total

    weight_sq = lax.fori_loop(0, rows // 8, weight_step, weight_sq)

    def dev_at(a, b):
        return spot(a, b) * 2 + core

    steps = (0, -1, 1, 2)

    def piece(zc, k):
        return g_all.at[zc, k]

    def part(zc, k, h):
        return g_all.at[zc, k, pl.ds(h * per, per)]

    def spread(zc, q):
        k = spot(steps[q], 0)
        send(piece(zc, k), piece(zc, k), ag_send.at[zc], r3.at[zc, q, 0], z, dev_at(0, 1))
        send(piece(zc, k), piece(zc, k), ag_send.at[zc], r3.at[zc, q, 1], z, dev_at(0, -1))

    @pl.loop(0, NZ + 6)
    def _(it):
        @pl.when(it < NZ)
        def _():
            zc = column(it)

            @pl.when(it == 0)
            def _():
                arrived(
                    g_all.at[zc, chip, pl.ds((1 - core) * per, per)], gz_recv.at[zc, 1 - core]
                )

            @pl.when(it > 0)
            def _():
                for cc in range(2):
                    arrived(g_all.at[zc, chip, pl.ds(cc * per, per)], gz_recv.at[zc, cc])

            send(piece(zc, chip), piece(zc, chip), ag_send.at[zc], r1.at[zc, 0], z, dev_at(1, 0))
            send(piece(zc, chip), piece(zc, chip), ag_send.at[zc], r1.at[zc, 1], z, dev_at(-1, 0))
            spread(zc, 0)

        @pl.when((it >= 1) & (it < NZ + 1))
        def _():
            zc = column(it - 1)
            k = spot(-1, 0)
            arrived(piece(zc, k), r1.at[zc, 0])
            send(part(zc, k, 0), part(zc, k, 0), ag_send.at[zc], r2.at[zc, 0], z, dev_at(1, 0))
            spread(zc, 1)
            k = spot(1, 0)
            arrived(piece(zc, k), r1.at[zc, 1])
            send(part(zc, k, 1), part(zc, k, 1), ag_send.at[zc], r2.at[zc, 1], z, dev_at(-1, 0))
            spread(zc, 2)

        @pl.when((it >= 2) & (it < NZ + 2))
        def _():
            zc = column(it - 2)
            k = spot(2, 0)
            for h in range(2):
                arrived(part(zc, k, h), r2.at[zc, h])
            spread(zc, 3)

        @pl.when((it >= 3) & (it < NZ + 3))
        def _():
            zc = column(it - 3)
            for q in range(4):
                k = spot(steps[q], -1)
                arrived(piece(zc, k), r3.at[zc, q, 0])
                send(part(zc, k, 0), part(zc, k, 0), ag_send.at[zc], r4.at[zc, q, 0], z, dev_at(0, 1))
                k = spot(steps[q], 1)
                arrived(piece(zc, k), r3.at[zc, q, 1])
                send(part(zc, k, 1), part(zc, k, 1), ag_send.at[zc], r4.at[zc, q, 1], z, dev_at(0, -1))

        @pl.when((it >= 4) & (it < NZ + 4))
        def _():
            zc = column(it - 4)
            for q in range(4):
                k = spot(steps[q], 2)
                for h in range(2):
                    arrived(part(zc, k, h), r4.at[zc, q, h])

            @pl.when(it > 4)
            def _():
                arrived(x_all.at[zc, core], xz_recv.at[zc])
                send(x_all.at[zc, core], x_all.at[zc, core], xp_send, xp_recv.at[zc], z, pal)

        @pl.when(it >= 6)
        def _():
            zc = column(it - 6)
            arrived(x_all.at[zc, 1 - core], xp_recv.at[zc])
            for cc in range(2):
                x_turn[cc * rows : (cc + 1) * rows, :] = x_all[zc, cc].T

            @pl.loop(0, half // 256)
            def _(n):
                where = pl.ds(pl.multiple_of(n * 256, 256), 256)
                block = g_all[zc, :, :, where].reshape(tokens, 256)
                acc[:, where] += jnp.dot(
                    x_turn[...], block, preferred_element_type=jnp.float32
                )

    send(
        acc.at[pl.ds((1 - core) * rows, rows)],
        grad.at[:, pl.ds(core * half, half)],
        half_send,
        half_recv,
        z,
        pal,
    )

    def grad_step(i, total):
        v = acc[pl.ds(pl.multiple_of(i * 8, 8), 8), :]
        v = v * v
        for k in range(half // 128):
            total = total + v[:, k * 128 : (k + 1) * 128]
        return total

    grad_sq = lax.fori_loop(0, 2 * rows // 8, grad_step, jnp.zeros((8, 128), jnp.float32))
    norms[d, 0] = weight_sq
    norms[d, 1] = grad_sq

    @pl.loop(1, ND)
    def _(p):
        send(norms.at[d], norms.at[d], norm_send, norm_recv.at[d], z, (d + p) % ND)

    grad[:, pl.ds(core * half, half)] = acc[pl.ds(core * rows, rows), :]
    m_load.wait()

    @pl.loop(1, ND)
    def _(p):
        j = (d + p) % ND
        arrived(norms.at[j], norm_recv.at[j])

    totals = jnp.sum(norms[...], axis=0)
    weight_total = jnp.sum(totals[0], keepdims=True)
    grad_total = jnp.sum(totals[1], keepdims=True)
    weight_norm = jnp.sqrt(weight_total + eps_norm)
    trust = weight_norm / (jnp.sqrt(grad_total + eps_norm) + tower_decay * weight_norm)
    scale = tower_rate * trust
    arrived(grad.at[:, pl.ds((1 - core) * half, half)], half_recv)

    strip = 16
    cut = rows // 2

    def slab(s, h):
        return slabs.at[s, pl.ds(h * cut, cut)]

    for h in range(2):

        @pl.loop(0, cut // strip)
        def _(i):
            at = pl.ds(pl.multiple_of(h * cut + i * strip, strip), strip)
            old = w[at, :]
            new_m = momentum_keep * m[at, :] + scale * (grad[at, :] + tower_decay * old)
            new_w = old - new_m
            m[at, :] = new_m
            w[at, :] = new_w
            slabs[z, at, :] = new_w.astype(jnp.bfloat16)

        send(slab(z, h), slab(z, h), wz_send, wz_recv.at[0, 0, h], (z + 1) % NZ, d)
        send(slab(z, h), slab(z, h), wz_send, wz_recv.at[1, 0, h], (z + NZ - 1) % NZ, d)

    @pl.loop(1, ND)
    def _(p):
        j = (d + p) % ND
        send(
            bg_hbm.at[0, 0, pl.ds(2 * j, 2)],
            got.at[pl.ds(2 * d, 2)],
            bg_send,
            bg_recv.at[d],
            z,
            j,
        )
        send(tag.at[j], got_tag.at[d], tag_send, tag_recv.at[d], z, j)

    w_store = pltpu.make_async_copy(w, w_out.at[0], out_sem.at[0])
    m_store = pltpu.make_async_copy(m, m_out.at[0], out_sem.at[1])
    w_store.start()
    m_store.start()
    pltpu.make_async_copy(slabs.at[z], slots_out.at[z], slab_sem).start()

    for j in range(1, 4):
        low = (z + NZ - j) % NZ
        high = (z + j) % NZ
        for h in range(2):
            arrived(slab(low, h), wz_recv.at[0, j - 1, h])
            if j < 3 or h == 0:
                send(slab(low, h), slab(low, h), wz_send, wz_recv.at[0, j, h], (z + 1) % NZ, d)
            arrived(slab(high, h), wz_recv.at[1, j - 1, h])
            if j < 3 or h == 1:
                send(slab(high, h), slab(high, h), wz_send, wz_recv.at[1, j, h], (z + NZ - 1) % NZ, d)
        pltpu.make_async_copy(slabs.at[low], slots_out.at[low], slab_sem).start()
        pltpu.make_async_copy(slabs.at[high], slots_out.at[high], slab_sem).start()

    own_load.wait()
    t_load.wait()

    @pl.loop(1, ND)
    def _(p):
        j = (d + p) % ND
        arrived(got.at[pl.ds(2 * j, 2)], bg_recv.at[j])
        arrived(got_tag.at[j], tag_recv.at[j])

    nb = table.shape[0]
    wide = table.shape[2]

    @pl.loop(0, table.shape[1] // strip)
    def _(i):
        at = pl.ds(pl.multiple_of(i * strip, strip), strip)

        def add(s, totals):
            totals = list(totals)
            for r in range(2):
                name = got_tag[s, r : r + 1, :]
                value = got[2 * s + r, at, :].astype(jnp.float32)
                for b in range(nb):
                    totals[b] = totals[b] + jnp.where(name == b, value, 0.0)
            return tuple(totals)

        totals = lax.fori_loop(
            0, ND, add, tuple(jnp.zeros((strip, wide), jnp.float32) for _ in range(nb))
        )
        for b in range(nb):
            sums[b, at, :] = totals[b]

    names = got_tag[:, 0:2, :]
    for b in range(nb):
        hits = jnp.sum(jnp.where(names == b, 1.0, 0.0), axis=(0, 1)).reshape(1, wide)
        flat = table[b]
        total = sums[b]
        w_norm = jnp.sqrt(jnp.sum(flat * flat, keepdims=True) + eps_norm)
        g_norm = jnp.sqrt(jnp.sum(total * total, keepdims=True) + eps_norm)
        block_trust = w_norm / (g_norm + table_decay * w_norm)
        moved = flat - table_rate * block_trust * (total + table_decay * flat)
        table[b] = jnp.where(hits > 0, moved, flat)
    t_store = pltpu.make_async_copy(table, t_out.at[0], out_sem.at[2])
    t_store.start()

    far = (z + 4) % NZ
    arrived(slab(far, 0), wz_recv.at[0, 3, 0])
    arrived(slab(far, 1), wz_recv.at[1, 3, 1])
    pltpu.make_async_copy(slabs.at[far], slots_out.at[far], slab_sem).start()

    arrived(g_slot.at[0, 0], gz_send.at[1])
    arrived(g_slot.at[:, 0:7], gz_send.at[0])
    arrived(x_slot.at[0:7], xz_send)
    arrived(x_slot, xp_send)

    @pl.loop(0, NZ)
    def _(k):
        arrived(g_all.at[k, 0 : NCHIP - 1], ag_send.at[k])

    arrived(acc.at[0:rows], half_send)
    arrived(norms.at[0 : ND - 1], norm_send)
    arrived(got.at[0 : 2 * (ND - 1)], bg_send)
    arrived(tag.at[0 : ND - 1], tag_send)
    arrived(slabs.at[0:7], wz_send)
    w_store.wait()
    m_store.wait()
    t_store.wait()
    pltpu.make_async_copy(slabs, slots_out, slab_sem).wait()


def finish_kernel(owner, slots, new_w, new_m, new_t, out, w_out, m_out, t_out):
    out[...] = slots[...]
    w_out[...] = new_w[...]
    m_out[...] = new_m[...]
    t_out[...] = new_t[...]


def local(
    layer_inputs,
    output_grads,
    layer_owner,
    master_weights,
    momentum,
    table_blocks,
    block_grads,
    block_ids,
    block_counts,
):
    layers, tokens, rows = layer_inputs.shape
    per, cols = output_grads.shape[1:]
    half = cols // 2
    nb, tall, wide = table_blocks.shape[1:]
    f32, bf16, i32 = jnp.float32, jnp.bfloat16, jnp.int32
    hbm = pl.BlockSpec(memory_space=pltpu.HBM)
    smem = pl.BlockSpec(memory_space=pltpu.SMEM)
    dma = pltpu.SemaphoreType.DMA
    slots, new_w, new_m, new_t = pl.pallas_call(
        step_kernel,
        name="step",
        out_shape=(
            jax.ShapeDtypeStruct((NZ, rows, cols), bf16),
            jax.ShapeDtypeStruct(master_weights.shape, f32),
            jax.ShapeDtypeStruct(momentum.shape, f32),
            jax.ShapeDtypeStruct(table_blocks.shape, f32),
        ),
        in_specs=[smem, smem, smem] + [hbm] * 6,
        out_specs=(hbm, hbm, hbm, hbm),
        scratch_shapes=[
            pltpu.VMEM((layers, tokens, rows), bf16),
            pltpu.VMEM((layers, tokens, rows), bf16),
            pltpu.VMEM((NZ, 2, tokens, rows), bf16),
            pltpu.VMEM((2 * rows, tokens), bf16),
            pltpu.VMEM((layers, per, cols), bf16),
            pltpu.VMEM((2, layers, per, half), bf16),
            pltpu.VMEM((NZ, NCHIP, 2 * per, half), bf16),
            pltpu.VMEM((2 * rows, half), f32),
            pltpu.VMEM((rows, cols), f32),
            pltpu.VMEM((rows, cols), f32),
            pltpu.VMEM((rows, cols), f32),
            pltpu.VMEM((nb, tall, wide), f32),
            pltpu.VMEM((nb, tall, wide), f32),
            pltpu.VMEM((2 * ND, tall, wide), bf16),
            pltpu.VMEM((ND, 8, wide), i32),
            pltpu.VMEM((ND, 8, wide), i32),
            pltpu.VMEM((ND, 2, 8, 128), f32),
            pltpu.VMEM((NZ, rows, cols), bf16),
            dma((5,)),
            dma((3,)),
            dma((2,)),
            dma((NZ, 2)),
            dma,
            dma((NZ,)),
            dma,
            dma((NZ,)),
            dma((NZ,)),
            dma((NZ, 2)),
            dma((NZ, 2)),
            dma((NZ, 4, 2)),
            dma((NZ, 4, 2)),
            dma,
            dma,
            dma,
            dma((ND,)),
            dma,
            dma((ND,)),
            dma,
            dma((ND,)),
            dma,
            dma,
            dma((2, 4, 2)),
            dma,
        ],
        compiler_params=pltpu.CompilerParams(
            collective_id=0, has_side_effects=True, vmem_limit_bytes=60 * 1024 * 1024
        ),
    )(
        layer_owner,
        block_ids,
        block_counts,
        layer_inputs,
        output_grads,
        master_weights,
        momentum,
        table_blocks,
        block_grads,
    )
    share = rows // layers
    by_rows = pl.BlockSpec((1, share, cols), lambda l, owner: (0, l, 0))
    by_block = pl.BlockSpec((1, nb // layers, tall, wide), lambda l, owner: (0, l, 0, 0))
    new_weights, new_master, new_moment, new_table = pl.pallas_call(
        finish_kernel,
        name="finish",
        grid_spec=pltpu.PrefetchScalarGridSpec(
            num_scalar_prefetch=1,
            grid=(layers,),
            in_specs=[
                pl.BlockSpec((1, rows, cols), lambda l, owner: (owner[l], 0, 0)),
                by_rows,
                by_rows,
                by_block,
            ],
            out_specs=[
                pl.BlockSpec((1, rows, cols), lambda l, owner: (l, 0, 0)),
                by_rows,
                by_rows,
                by_block,
            ],
        ),
        out_shape=(
            jax.ShapeDtypeStruct((layers, rows, cols), bf16),
            jax.ShapeDtypeStruct(master_weights.shape, f32),
            jax.ShapeDtypeStruct(momentum.shape, f32),
            jax.ShapeDtypeStruct(table_blocks.shape, f32),
        ),
    )(layer_owner, slots, new_w, new_m, new_t)
    return new_master, new_moment, new_weights, new_table


def solution(mesh):
    return jax.shard_map(
        local,
        mesh=mesh,
        in_specs=(
            P(None, "grp", "dev"),
            P(None, ("grp", "dev"), None),
            P(),
            P("grp", "dev", None),
            P("grp", "dev", None),
            P("grp", "dev", None, None),
            P("grp", "dev", None, None, None),
            P("grp", "dev", None),
            P("grp", "dev", None),
        ),
        out_specs=(
            P("grp", "dev", None),
            P("grp", "dev", None),
            P(None, "dev", None),
            P("grp", "dev", None, None),
        ),
        check_vma=False,
    )
```

profile of v0, /device:TPU:1, one launch (start us, length us, event | category | flops | bytes accessed | tf_op | source)
XLA Modules:
  0.0 167.6 jit_solution(4059381749842205382)
XLA Ops:
  0.6 158.3 %step.1 = (bf16[8,128,2048]{2,1,0:T(8,128)(2,1)}, f32[1,128,2048]{2,1,0:T(8,128)}, f32[1,128,2048]{2,1,0:T(8,128)}, f32[1,8,128,128]{3,2,1,0:T(8,128)}) custom-call(s32[8]{0:T(128)} %owner.3, s32[1,1,64]{2,1,0:T(1,128)} %ids.1, s32[1,1,32]{2,1,0:T(1,128)} %counts.1, bf16[8,1024,128]{2,1,0:T(8,128)(2,1)} %x_hbm.1, bf16[8,32,2048]{2,1,0:T(8,128)(2,1)} %g_hbm.1, ...), custom_call_target="tpu_custom_call" | custom-call | tf_op jit(solution)/shard_map/step/pallas_call | solution.py:510
  159.0 8.6 %finish.1 = (bf16[8,128,2048]{2,1,0:T(8,128)(2,1)}, f32[1,128,2048]{2,1,0:T(8,128)}, f32[1,128,2048]{2,1,0:T(8,128)}, f32[1,8,128,128]{3,2,1,0:T(8,128)}) custom-call(s32[8]{0:T(128)} %owner.3, bf16[8,128,2048]{2,1,0:T(8,128)(2,1)} %get-tuple-element.12.slots, f32[1,128,2048]{2,1,0:T(8,128)} %get-tuple-element.13.new_w, ...), custom_call_target="tpu_custom_call" | custom-call | tf_op jit(solution)/shard_map/finish/pallas_call | solution.py:583
where the time goes:
time: 168 us
  Pallas kernels  167 us (99%)
    pallas_call x1, Pallas kernels, local(): pl.pallas_call(step_kernel, name='step', out_shape=(jax.ShapeDtypeStruct(...  158 us
    pallas_call x1, Pallas kernels, local(): pl.pallas_call(finish_kernel, name='finish', grid_spec=pltpu.PrefetchScal...  8.61 us

commit v1 on v0

v1 whole, which is shorter than its diff:
```python
import functools

import jax
import jax.numpy as jnp
from jax import lax
from jax.experimental import pallas as pl
from jax.experimental.pallas import tpu as pltpu
from jax.sharding import PartitionSpec as P

tower_rate = 0.5
momentum_keep = 0.9
tower_decay = 0.1
table_rate = 0.5
table_decay = 0.2
eps_norm = 1e-06

NZ = 8
NX = 4
NY = 4
ND = NX * NY * 2


def step_kernel(
    owner,
    ids,
    counts,
    x_hbm,
    g_hbm,
    w_hbm,
    m_hbm,
    t_hbm,
    bg_hbm,
    slabs,
    w,
    m,
    table,
    x_in,
    x_slot,
    x_all,
    x_turn,
    x_relay,
    g_in,
    g_slot,
    g_all,
    g_relay,
    acc,
    grad,
    sums,
    pick,
    turned,
    got,
    tag,
    got_tag,
    norms,
    in_sem,
    gz_send,
    gz_recv,
    go_send,
    gr_send,
    gr_recv,
    gf_send,
    xz_send,
    xz_recv,
    xr_send,
    xr_recv,
    xf_send,
    xo_send,
    xo_recv,
    xp_send,
    xp_recv,
    ag_send,
    ag_recv,
    half_send,
    half_recv,
    norm_send,
    norm_recv,
    bg_send,
    bg_recv,
    tag_send,
    tag_recv,
    wz_send,
    wz_recv,
):
    z = lax.axis_index("grp")
    d = lax.axis_index("dev")
    core = d % 2
    cx = (d // 2) % NX
    cy = d // (2 * NX)
    chip = d // 2
    side = cy // 2
    duo = ((cy + 1) // 2) % 2
    oy = NY - 1 - cy
    iy = cy + 1 - 2 * (cy % 2)
    me = side * 2 + core
    pal = chip * 2 + 1 - core
    outer = (oy * NX + cx) * 2 + core
    inner = (iy * NX + cx) * 2 + core
    right = (cy * NX + (cx + 1) % NX) * 2 + core
    left = (cy * NX + (cx + NX - 1) % NX) * 2 + core
    rows = w_hbm.shape[1]
    cols = w_hbm.shape[2]
    quarter = cols // 4
    per = g_hbm.shape[1]
    tokens = x_hbm.shape[1]
    band = tokens // NY

    def send(src, dst, s_sem, r_sem, zz, dd):
        pltpu.make_async_remote_copy(
            src_ref=src,
            dst_ref=dst,
            send_sem=s_sem,
            recv_sem=r_sem,
            device_id=(zz, dd),
            device_id_type=pl.DeviceIdType.MESH,
        ).start()

    def arrived(ref, sem):
        pltpu.make_async_copy(ref, ref, sem).wait()

    def column(i):
        off = (i % 2) * ((i + 1) // 2) + (1 - i % 2) * (NZ - i // 2)
        return (z + off) % NZ

    def holder(p, cc):
        y = jnp.where(p == side, cy, oy)
        return (y * NX + cx) * 2 + cc

    g_load = pltpu.make_async_copy(g_hbm, g_in, in_sem.at[1])
    x_load = pltpu.make_async_copy(x_hbm, x_in, in_sem.at[0])
    w_load = pltpu.make_async_copy(w_hbm.at[0], w.at[0], in_sem.at[2])
    m_load = pltpu.make_async_copy(m_hbm.at[0], m.at[0], in_sem.at[3])
    t_load = pltpu.make_async_copy(t_hbm.at[0], table.at[0], in_sem.at[4])
    own_load = pltpu.make_async_copy(
        bg_hbm.at[0, 0, pl.ds(2 * d, 2)], got.at[pl.ds(2 * d, 2)], in_sem.at[5]
    )
    g_load.start()
    x_load.start()
    w_load.start()
    m_load.start()
    t_load.start()
    own_load.start()

    barrier = pltpu.get_barrier_semaphore()

    @pl.loop(1, ND)
    def _(p):
        pl.semaphore_signal(
            barrier, inc=1, device_id=(z, (d + p) % ND), device_id_type=pl.DeviceIdType.MESH
        )

    @pl.loop(1, NZ)
    def _(p):
        for ps in range(2):
            for cc in range(2):
                pl.semaphore_signal(
                    barrier,
                    inc=1,
                    device_id=((z + p) % NZ, holder(ps, cc)),
                    device_id_type=pl.DeviceIdType.MESH,
                )

    def layer_of(s):
        found = jnp.int32(0)
        for l in range(NZ):
            found = jnp.where(owner[l] == s, l, found)
        return found
    g_load.wait()

    @pl.loop(0, NZ)
    def _(s):
        l = layer_of(s)
        for q in range(4):
            g_slot[s, q] = g_in[l, :, q * quarter : (q + 1) * quarter]

    g_all[z, duo, side, cx, pl.ds(core * per, per), :] = g_slot[z, me]
    x_load.wait()

    @pl.loop(0, NZ)
    def _(s):
        l = layer_of(s)
        x_slot[s] = x_in[l]

    x_all[z, me] = x_slot[z]
    pl.semaphore_wait(barrier, ND - 1 + 4 * (NZ - 1))
    def g_home(zs):
        return g_all.at[zs, duo, side, cx, pl.ds(core * per, per)]

    far = (z + NZ // 2) % NZ
    ways = (1, NZ - 1)
    deep = tokens // 2
    for way in range(2):
        zn = (z + ways[way]) % NZ
        send(g_slot.at[far, 2 * way : 2 * way + 2], g_relay.at[way], gr_send, gr_recv.at[way], zn, d)
        send(
            x_slot.at[far, way * deep : (way + 1) * deep],
            x_relay.at[way],
            xr_send,
            xr_recv.at[way],
            zn,
            d,
        )
    send(g_slot.at[z, side * 2 + 1 - core], g_home(z), go_send.at[0], gz_recv.at[z, me], z, pal)
    for cc in range(2):
        send(
            g_slot.at[z, (1 - side) * 2 + cc],
            g_home(z),
            go_send.at[1 + cc],
            gz_recv.at[z, me],
            z,
            (oy * NX + cx) * 2 + cc,
        )

    def g_out(i):
        zt = column(i)
        for ps in range(2):
            for cc in range(2):
                send(
                    g_slot.at[zt, 2 * ps + cc],
                    g_home(z),
                    gz_send,
                    gz_recv.at[z, me],
                    zt,
                    holder(ps, cc),
                )

    def x_out(i):
        zt = column(i)
        send(x_slot.at[zt], x_all.at[z, me], xz_send, xz_recv.at[z, 0], zt, d)

    def x_share(ref, zs, h):
        send(ref, ref, xo_send, xo_recv.at[zs, h], z, outer)
        send(ref, ref, xp_send, xp_recv.at[zs, 0, h], z, pal)

    def x_half(zs, s, h):
        return x_all.at[zs, s, pl.ds(h * deep, deep)]

    @pl.loop(1, 5)
    def _(i):
        g_out(i)

    @pl.loop(1, 3)
    def _(i):
        x_out(i)

    @pl.loop(5, 7)
    def _(i):
        g_out(i)

    @pl.loop(3, 5)
    def _(i):
        x_out(i)

    x_share(x_all.at[z, me], z, 0)

    def whole(zs, pr, da):
        return g_all.at[zs, pr, :, (cx + da + NX) % NX]

    def part(zs, pr, da, h):
        return g_all.at[zs, pr, h, (cx + da + NX) % NX]

    def push(ref, zs, k, dd):
        send(ref, ref, ag_send, ag_recv.at[zs, k], z, dd)

    def landed(it):
        zs = column(it)

        @pl.when(it == 0)
        def _():
            for j, who in enumerate((pal, (oy * NX + cx) * 2, (oy * NX + cx) * 2 + 1)):
                wy = who // (2 * NX)
                wc = who % 2
                arrived(
                    g_all.at[z, duo, wy // 2, cx, pl.ds(wc * per, per)],
                    gz_recv.at[z, (wy // 2) * 2 + wc],
                )

        @pl.when(it > 0)
        def _():
            for ps in range(2):
                for cc in range(2):
                    arrived(
                        g_all.at[zs, duo, ps, cx, pl.ds(cc * per, per)],
                        gz_recv.at[zs, 2 * ps + cc],
                    )

    def relay():
        for way in range(2):
            zs = (z + NZ - ways[way]) % NZ
            zt = (zs + NZ // 2) % NZ
            arrived(g_relay.at[way], gr_recv.at[way])
            for cc in range(2):
                send(
                    g_relay.at[way, cc], g_home(zs), gf_send, gz_recv.at[zs, me], zt, holder(way, cc)
                )

        @pl.loop(5, 7)
        def _(i):
            x_out(i)

        for way in range(2):
            zs = (z + NZ - ways[way]) % NZ
            zt = (zs + NZ // 2) % NZ
            arrived(x_relay.at[way], xr_recv.at[way])
            send(
                x_relay.at[way],
                x_all.at[zs, me, pl.ds(way * deep, deep)],
                xf_send,
                xz_recv.at[zs, way],
                zt,
                d,
            )

    there = (1 - side) * 2 + core

    def x_stages(it):
        lag = jnp.where(it < NZ, 0, 2)

        @pl.when(((it >= 3) & (it < 7)) | ((it >= 9) & (it < 11)))
        def _():
            zs = column(it - 2 - lag)
            arrived(x_all.at[zs, me], xz_recv.at[zs, 0])
            x_share(x_all.at[zs, me], zs, 0)

        @pl.when(it == 11)
        def _():
            zs = column(NZ - 1)
            for h in range(2):
                arrived(x_half(zs, me, h), xz_recv.at[zs, h])
                x_share(x_half(zs, me, h), zs, h)

        lead = jnp.where(it < 9, 0, 2)

        @pl.when(((it >= 4) & (it < 9)) | (it >= 11))
        def _():
            zs = column(it - 4 - lead)

            @pl.when(it < NZ + 5)
            def _():
                for sd in range(2):
                    arrived(
                        x_all.at[zs, sd * 2 + 1 - core],
                        xp_recv.at[zs, jnp.where(sd == side, 0, 1), 0],
                    )

            @pl.when(it == NZ + 5)
            def _():
                for h in range(2):
                    for sd in range(2):
                        arrived(
                            x_half(zs, sd * 2 + 1 - core, h),
                            xp_recv.at[zs, jnp.where(sd == side, 0, 1), h],
                        )
            @pl.loop(0, 4)
            def _(s):
                for y in range(NY):
                    order = ((y + 1) // 2) % 2 * 2 + y // 2
                    x_turn[pl.ds(s * rows, rows), order * band : (order + 1) * band] = x_all[
                        zs, s, y * band : (y + 1) * band, :
                    ].T

            @pl.loop(0, quarter // 256)
            def _(n):
                where = pl.ds(pl.multiple_of(n * 256, 256), 256)
                block = g_all[zs, :, :, :, :, where].reshape(tokens, 256)
                acc[:, where] += jnp.dot(x_turn[...], block, preferred_element_type=jnp.float32)

        @pl.when(((it >= 3) & (it < 8)) | ((it >= 10) & (it < 12)))
        def _():
            zs = column(it - 3 - jnp.where(it < 8, 0, 2))
            arrived(x_all.at[zs, there], xo_recv.at[zs, 0])
            send(x_all.at[zs, there], x_all.at[zs, there], xp_send, xp_recv.at[zs, 1, 0], z, pal)

        @pl.when(it == 12)
        def _():
            zs = column(NZ - 1)
            for h in range(2):
                arrived(x_half(zs, there, h), xo_recv.at[zs, h])
                send(x_half(zs, there, h), x_half(zs, there, h), xp_send, xp_recv.at[zs, 1, h], z, pal)
    @pl.loop(0, ND)
    def _(j):
        for r in range(2):
            t = jnp.where(r < counts[0, 0, j], ids[0, 0, 2 * j + r], -1)
            tag[j, r : r + 1, :] = jnp.full((1, tag.shape[2]), t, jnp.int32)

    got_tag[d] = tag[d]
    acc[...] = jnp.zeros_like(acc)
    w_load.wait()

    def weight_step(i, total):
        v = w[0, pl.ds(pl.multiple_of(i * 8, 8), 8), :]
        v = v * v
        for k in range(cols // 128):
            total = total + v[:, k * 128 : (k + 1) * 128]
        return total

    weight_sq = lax.fori_loop(0, rows // 8, weight_step, jnp.zeros((8, 128), jnp.float32))
    @pl.when(core == 0)
    def _():
        @pl.loop(0, NZ + 6)
        def _(it):
            @pl.when(it < NZ)
            def _():
                zs = column(it)
                landed(it)
                push(whole(zs, duo, 0), zs, 0, right)
                push(whole(zs, duo, 0), zs, 1, left)
                push(whole(zs, duo, 0), zs, 4, inner)

            @pl.when(it == 1)
            def _():
                relay()

            @pl.when((it >= 1) & (it < NZ + 1))
            def _():
                zs = column(it - 1)
                arrived(whole(zs, duo, -1), ag_recv.at[zs, 0])
                push(part(zs, duo, -1, 0), zs, 2, right)
                push(whole(zs, duo, -1), zs, 5, inner)
                arrived(whole(zs, duo, 1), ag_recv.at[zs, 1])
                push(part(zs, duo, 1, 1), zs, 3, left)
                push(whole(zs, duo, 1), zs, 6, inner)

            @pl.when((it >= 2) & (it < NZ + 2))
            def _():
                zs = column(it - 2)
                for h in range(2):
                    arrived(part(zs, duo, 2, h), ag_recv.at[zs, 2 + h])
                push(whole(zs, duo, 2), zs, 7, inner)

            @pl.when((it >= 3) & (it < NZ + 3))
            def _():
                zs = column(it - 3)
                for k, da in enumerate((0, -1, 1, 2)):
                    arrived(whole(zs, 1 - duo, da), ag_recv.at[zs, 4 + k])

            x_stages(it)

    @pl.when(core == 1)
    def _():
        @pl.loop(0, NZ + 6)
        def _(it):
            @pl.when(it < NZ)
            def _():
                zs = column(it)
                landed(it)
                push(whole(zs, duo, 0), zs, 4, inner)
                push(whole(zs, duo, 0), zs, 0, right)
                push(whole(zs, duo, 0), zs, 1, left)

            @pl.when(it == 1)
            def _():
                relay()

            @pl.when((it >= 1) & (it < NZ + 1))
            def _():
                zs = column(it - 1)
                arrived(whole(zs, 1 - duo, 0), ag_recv.at[zs, 4])
                push(whole(zs, 1 - duo, 0), zs, 5, right)
                push(whole(zs, 1 - duo, 0), zs, 6, left)
                arrived(whole(zs, duo, -1), ag_recv.at[zs, 0])
                push(part(zs, duo, -1, 0), zs, 2, right)
                arrived(whole(zs, duo, 1), ag_recv.at[zs, 1])
                push(part(zs, duo, 1, 1), zs, 3, left)

            @pl.when((it >= 2) & (it < NZ + 2))
            def _():
                zs = column(it - 2)
                arrived(whole(zs, 1 - duo, -1), ag_recv.at[zs, 5])
                push(part(zs, 1 - duo, -1, 0), zs, 7, right)
                arrived(whole(zs, 1 - duo, 1), ag_recv.at[zs, 6])
                push(part(zs, 1 - duo, 1, 1), zs, 8, left)
                for h in range(2):
                    arrived(part(zs, duo, 2, h), ag_recv.at[zs, 2 + h])

            @pl.when((it >= 3) & (it < NZ + 3))
            def _():
                zs = column(it - 3)
                for h in range(2):
                    arrived(part(zs, 1 - duo, 2, h), ag_recv.at[zs, 7 + h])

            x_stages(it)
    def grad_step(i, total):
        v = acc[pl.ds(pl.multiple_of(i * 8, 8), 8), :]
        v = v * v
        for k in range(quarter // 128):
            total = total + v[:, k * 128 : (k + 1) * 128]
        return total

    grad_sq = lax.fori_loop(0, 4 * rows // 8, grad_step, jnp.zeros((8, 128), jnp.float32))
    norms[d, 0:1] = jnp.sum(weight_sq, axis=0, keepdims=True)
    norms[d, 1:2] = jnp.sum(grad_sq, axis=0, keepdims=True)

    grad[:, pl.ds(pl.multiple_of(me * quarter, quarter), quarter)] = acc[pl.ds(me * rows, rows), :]

    @pl.loop(1, ND)
    def _(p):
        send(norms.at[d], norms.at[d], norm_send, norm_recv.at[d], z, (d + p) % ND)
    mates = (
        (me, d),
        (side * 2 + 1 - core, pal),
        ((1 - side) * 2 + core, outer),
        ((1 - side) * 2 + 1 - core, outer + 1 - 2 * core),
    )

    def columns(k):
        return pl.ds(pl.multiple_of(mates[k][0] * quarter, quarter), quarter)

    for k in range(1, 4):
        send(
            acc.at[pl.ds(mates[k][0] * rows, rows)],
            grad.at[:, columns(0)],
            half_send,
            half_recv.at[k - 1],
            z,
            mates[k][1],
        )

    def block_out(j):
        send(tag.at[j], got_tag.at[d], tag_send, tag_recv.at[d], z, j)
        send(
            bg_hbm.at[0, 0, pl.ds(2 * j, 2)],
            got.at[pl.ds(2 * d, 2)],
            bg_send,
            bg_recv.at[d],
            z,
            j,
        )

    near = ND // 2

    @pl.loop(1, near)
    def _(p):
        block_out(side * near + (d + p) % near)
    m_load.wait()

    @pl.loop(1, ND)
    def _(p):
        j = (d + p) % ND
        arrived(norms.at[j], norm_recv.at[j])
    totals = jnp.sum(norms[...], axis=0)
    weight_total = jnp.sum(totals[0:1], keepdims=True)
    grad_total = jnp.sum(totals[1:2], keepdims=True)
    weight_norm = jnp.sqrt(weight_total + eps_norm)
    trust = weight_norm / (jnp.sqrt(grad_total + eps_norm) + tower_decay * weight_norm)
    scale = tower_rate * trust

    strip = 16
    up = (z + 1) % NZ
    down = (z + NZ - 1) % NZ

    def piece(s, k):
        return slabs.at[s, :, columns(k)]

    def renew(k):
        @pl.loop(0, rows // strip)
        def _(i):
            at = pl.ds(pl.multiple_of(i * strip, strip), strip)
            old = w[0, at, columns(k)]
            new_m = momentum_keep * m[0, at, columns(k)] + scale * (
                grad[at, columns(k)] + tower_decay * old
            )
            new_w = old - new_m
            m[0, at, columns(k)] = new_m
            w[0, at, columns(k)] = new_w
            slabs[z, at, columns(k)] = new_w.astype(jnp.bfloat16)

        send(piece(z, k), piece(z, k), wz_send, wz_recv.at[0, 0, k], up, d)
        send(piece(z, k), piece(z, k), wz_send, wz_recv.at[1, 0, k], down, d)

    def onward(j, ks):
        low = (z + NZ - j) % NZ
        high = (z + j) % NZ
        for k in ks:
            if j < 3 or k % 2 == 0:
                arrived(piece(low, k), wz_recv.at[0, j - 1, k])
                send(piece(low, k), piece(low, k), wz_send, wz_recv.at[0, j, k], up, d)
            if j < 3 or k % 2 == 1:
                arrived(piece(high, k), wz_recv.at[1, j - 1, k])
                send(piece(high, k), piece(high, k), wz_send, wz_recv.at[1, j, k], down, d)
    renew(0)
    arrived(grad.at[:, columns(1)], half_recv.at[0])
    renew(1)
    onward(1, (0, 1))
    arrived(grad.at[:, columns(2)], half_recv.at[1])
    renew(2)
    onward(2, (0, 1))
    arrived(grad.at[:, columns(3)], half_recv.at[2])
    renew(3)
    @pl.loop(0, near)
    def _(p):
        block_out((1 - side) * near + (d + p) % near)
    onward(1, (2, 3))
    onward(3, (0, 1))
    onward(2, (2, 3))
    onward(3, (2, 3))
    own_load.wait()
    t_load.wait()

    @pl.loop(1, ND)
    def _(p):
        j = (d + p) % ND
        arrived(got.at[pl.ds(2 * j, 2)], bg_recv.at[j])
        arrived(got_tag.at[j], tag_recv.at[j])
    nb = table.shape[1]
    wide = table.shape[3]
    lane = lax.broadcasted_iota(jnp.int32, (strip, wide), 1)
    same = lane % strip == lax.broadcasted_iota(jnp.int32, (strip, wide), 0)
    names = lane // strip

    @pl.loop(0, ND)
    def _(s):
        for r in range(2):
            hit = (got_tag[s, r : r + 1, :] == names) & same
            pick[2 * s + r] = jnp.where(hit, 1.0, 0.0).astype(jnp.bfloat16)

    turned[...] = pick[...].reshape(2 * ND * strip, wide).T

    @pl.loop(0, table.shape[2] // strip)
    def _(i):
        at = pl.ds(pl.multiple_of(i * strip, strip), strip)
        values = got[:, at, :].reshape(2 * ND * strip, wide)
        total = jnp.dot(turned[...], values, preferred_element_type=jnp.float32)
        sums[:, at, :] = total.reshape(nb, strip, wide)

    tags = got_tag[:, 0:2, :]
    for b in range(nb):
        hits = jnp.sum(jnp.where(tags == b, 1.0, 0.0), axis=(0, 1)).reshape(1, wide)
        flat = table[0, b]
        total = sums[b]
        w_norm = jnp.sqrt(jnp.sum(flat * flat, keepdims=True) + eps_norm)
        g_norm = jnp.sqrt(jnp.sum(total * total, keepdims=True) + eps_norm)
        block_trust = w_norm / (g_norm + table_decay * w_norm)
        moved = flat - table_rate * block_trust * (total + table_decay * flat)
        table[0, b] = jnp.where(hits > 0, moved, flat)
    low = (z + NZ - 3) % NZ
    high = (z + 3) % NZ
    for k in range(4):
        if k % 2 == 0:
            arrived(piece(high, k), wz_recv.at[1, 2, k])
            arrived(piece(far, k), wz_recv.at[0, 3, k])
        else:
            arrived(piece(low, k), wz_recv.at[0, 2, k])
            arrived(piece(far, k), wz_recv.at[1, 3, k])
    arrived(g_slot.at[0:6], gz_send)
    for k in range(3):
        arrived(g_slot.at[0, 0], go_send.at[k])
    arrived(g_relay, gr_send)
    arrived(g_relay, gf_send)
    arrived(x_slot.at[0:6], xz_send)
    arrived(x_relay, xr_send)
    arrived(x_relay, xf_send)
    arrived(x_all.at[:, 0], xo_send)
    arrived(x_all.at[:, 0:2], xp_send)
    arrived(g_all.at[0:7], ag_send)
    arrived(acc.at[0 : 3 * rows], half_send)
    arrived(norms.at[0 : ND - 1], norm_send)
    arrived(got.at[0 : 2 * (ND - 1)], bg_send)
    arrived(tag.at[0 : ND - 1], tag_send)
    arrived(slabs.at[0:7], wz_send)


def finish_kernel(owner, slots, new_w, new_m, new_t, out, w_out, m_out, t_out, sem):
    copies = [
        pltpu.make_async_copy(slots.at[owner[l]], out.at[l], sem.at[l])
        for l in range(out.shape[0])
    ] + [
        pltpu.make_async_copy(new_w, w_out, sem.at[NZ]),
        pltpu.make_async_copy(new_m, m_out, sem.at[NZ + 1]),
        pltpu.make_async_copy(new_t, t_out, sem.at[NZ + 2]),
    ]
    for copy in copies:
        copy.start()
    for copy in copies:
        copy.wait()


def local(
    layer_inputs,
    output_grads,
    layer_owner,
    master_weights,
    momentum,
    table_blocks,
    block_grads,
    block_ids,
    block_counts,
):
    layers, tokens, rows = layer_inputs.shape
    per, cols = output_grads.shape[1:]
    quarter = cols // 4
    nb, tall, wide = table_blocks.shape[1:]
    f32, bf16, i32 = jnp.float32, jnp.bfloat16, jnp.int32
    hbm = pl.BlockSpec(memory_space=pltpu.HBM)
    smem = pl.BlockSpec(memory_space=pltpu.SMEM)
    anywhere = pl.BlockSpec(memory_space=pl.ANY)
    dma = pltpu.SemaphoreType.DMA
    slots, new_w, new_m, new_t = pl.pallas_call(
        step_kernel,
        name="step",
        out_shape=(
            pltpu.VMEM((NZ, rows, cols), bf16),
            pltpu.VMEM(master_weights.shape, f32),
            pltpu.VMEM(momentum.shape, f32),
            pltpu.VMEM(table_blocks.shape, f32),
        ),
        in_specs=[smem, smem, smem] + [hbm] * 6,
        out_specs=(pl.BlockSpec(memory_space=pltpu.VMEM),) * 4,
        scratch_shapes=[
            pltpu.VMEM((layers, tokens, rows), bf16),
            pltpu.VMEM((layers, tokens, rows), bf16),
            pltpu.VMEM((NZ, 4, tokens, rows), bf16),
            pltpu.VMEM((4 * rows, tokens), bf16),
            pltpu.VMEM((2, tokens // 2, rows), bf16),
            pltpu.VMEM((layers, per, cols), bf16),
            pltpu.VMEM((layers, 4, per, quarter), bf16),
            pltpu.VMEM((NZ, 2, 2, NX, 2 * per, quarter), bf16),
            pltpu.VMEM((2, 2, per, quarter), bf16),
            pltpu.VMEM((4 * rows, quarter), f32),
            pltpu.VMEM((rows, cols), f32),
            pltpu.VMEM((nb, tall, wide), f32),
            pltpu.VMEM((2 * ND, wide // nb, wide), bf16),
            pltpu.VMEM((wide, 2 * ND * (wide // nb)), bf16),
            pltpu.VMEM((2 * ND, tall, wide), bf16),
            pltpu.VMEM((ND, 8, wide), i32),
            pltpu.VMEM((ND, 8, wide), i32),
            pltpu.VMEM((ND, 2, 128), f32),
            dma((6,)),
            dma,
            dma((NZ, 4)),
            dma((3,)),
            dma,
            dma((2,)),
            dma,
            dma,
            dma((NZ, 2)),
            dma,
            dma((2,)),
            dma,
            dma,
            dma((NZ, 2)),
            dma,
            dma((NZ, 2, 2)),
            dma,
            dma((NZ, 9)),
            dma,
            dma((3,)),
            dma,
            dma((ND,)),
            dma,
            dma((ND,)),
            dma,
            dma((ND,)),
            dma,
            dma((2, 4, 4)),
        ],
        compiler_params=pltpu.CompilerParams(
            collective_id=0, has_side_effects=True, vmem_limit_bytes=60_160_000
        ),
    )(
        layer_owner,
        block_ids,
        block_counts,
        layer_inputs,
        output_grads,
        master_weights,
        momentum,
        table_blocks,
        block_grads,
    )
    new_weights, new_master, new_moment, new_table = pl.pallas_call(
        finish_kernel,
        name="finish",
        in_specs=[smem] + [anywhere] * 4,
        out_specs=(hbm,) * 4,
        scratch_shapes=[dma((layers + 3,))],
        out_shape=(
            jax.ShapeDtypeStruct((layers, rows, cols), bf16),
            jax.ShapeDtypeStruct(master_weights.shape, f32),
            jax.ShapeDtypeStruct(momentum.shape, f32),
            jax.ShapeDtypeStruct(table_blocks.shape, f32),
        ),
        compiler_params=pltpu.CompilerParams(vmem_limit_bytes=1024 * 1024),
    )(layer_owner, slots, new_w, new_m, new_t)
    return new_master, new_moment, new_weights, new_table


def solution(mesh):
    return jax.shard_map(
        local,
        mesh=mesh,
        in_specs=(
            P(None, "grp", "dev"),
            P(None, ("grp", "dev"), None),
            P(),
            P("grp", "dev", None),
            P("grp", "dev", None),
            P("grp", "dev", None, None),
            P("grp", "dev", None, None, None),
            P("grp", "dev", None),
            P("grp", "dev", None),
        ),
        out_specs=(
            P("grp", "dev", None),
            P("grp", "dev", None),
            P(None, "dev", None),
            P("grp", "dev", None, None),
        ),
        check_vma=False,
    )
```

time: 168 us -> 154 us (0.917)
  Pallas kernels: 167 us -> 153 us
    pallas_call x2, Pallas kernels: 167 us -> 153 us  [the longest x1 149 us: local(): pl.pallas_call(step_kernel, name='step', out_shape=(pltpu.VMEM((NZ, rows,...]
where the time goes in v1:
time: 154 us
  Pallas kernels  153 us (99%)
    pallas_call x1, Pallas kernels, local(): pl.pallas_call(step_kernel, name='step', out_shape=(pltpu.VMEM((NZ, rows,...  149 us
    pallas_call x1, Pallas kernels, local(): pl.pallas_call(finish_kernel, name='finish', in_specs=[smem] + [anywhere]...  3.45 us

profile of v1, /device:TPU:1, one launch (start us, length us, event | category | flops | bytes accessed | tf_op | source)
XLA Modules:
  0.0 153.5 jit_solution(12477349165980458423)
XLA Ops:
  0.6 0.0 copy-start
  0.6 149.4 %step.1 = (bf16[8,128,2048]{2,1,0:T(8,128)(2,1)S(1)}, f32[1,128,2048]{2,1,0:T(8,128)S(1)}, f32[1,128,2048]{2,1,0:T(8,128)S(1)}, f32[1,8,128,128]{3,2,1,0:T(8,128)S(1)}) custom-call(s32[8]{0:T(128)} %owner.3, s32[1,1,64]{2,1,0:T(1,128)} %ids.1, s32[1,1,32]{2,1,0:T(1,128)} %counts.1, bf16[8,1024,128]{2,1,0:T(8,128)(2,1)} %x_hbm.1, bf16[8,32,2048]{2,1,0:T(8,128)(2,1)} %g_hbm.1, ...), custom_call_target="tpu_custom_call" | custom-call | tf_op jit(solution)/shard_map/step/pallas_call | solution.py:697
  150.1 0.0 copy-done
  150.1 3.4 %finish.1 = (bf16[8,128,2048]{2,1,0:T(8,128)(2,1)}, f32[1,128,2048]{2,1,0:T(8,128)}, f32[1,128,2048]{2,1,0:T(8,128)}, f32[1,8,128,128]{3,2,1,0:T(8,128)}) custom-call(s32[8]{0:T(128)S(1)} %copy-done, bf16[8,128,2048]{2,1,0:T(8,128)(2,1)S(1)} %get-tuple-element.12.slots, f32[1,128,2048]{2,1,0:T(8,128)S(1)} %get-tuple-element.13.new_w, ...), custom_call_target="tpu_custom_call" | custom-call | tf_op jit(solution)/shard_map/finish/pallas_call | solution.py:770
Async XLA Ops:
  0.6 149.4 %copy-start = (s32[8]{0:T(128)S(1)}, s32[8]{0:T(128)}, u32[]{:S(2)}) copy-start(s32[8]{0:T(128)} %owner.3) | copy-start | bytes 100

commit v2 on v1

v2 whole, which is shorter than its diff:
```python
import functools

import jax
import jax.numpy as jnp
from jax import lax
from jax.experimental import pallas as pl
from jax.experimental.pallas import tpu as pltpu
from jax.sharding import PartitionSpec as P

tower_rate = 0.5
momentum_keep = 0.9
tower_decay = 0.1
table_rate = 0.5
table_decay = 0.2
eps_norm = 1e-06

NZ = 8
NX = 4
NY = 4
ND = NX * NY * 2


def step_kernel(
    owner,
    ids,
    counts,
    x_hbm,
    g_hbm,
    w_hbm,
    m_hbm,
    t_hbm,
    bg_hbm,
    slabs,
    w,
    m,
    table,
    x_in,
    x_slot,
    x_all,
    x_turn,
    x_relay,
    g_in,
    g_slot,
    g_other,
    g_all,
    g_relay,
    acc,
    grad,
    sums,
    pick,
    turned,
    got,
    tag,
    got_tag,
    norms,
    in_sem,
    gz_send,
    gz_recv,
    go_send,
    gx_send,
    gx_recv,
    gr_send,
    gr_recv,
    gf_send,
    xz_send,
    xz_recv,
    xr_send,
    xr_recv,
    xf_send,
    xo_send,
    xo_recv,
    xp_send,
    xp_recv,
    ag_send,
    ag_recv,
    half_send,
    half_recv,
    norm_send,
    norm_recv,
    bg_send,
    bg_recv,
    tag_send,
    tag_recv,
    wz_send,
    wz_recv,
):
    z = lax.axis_index("grp")
    d = lax.axis_index("dev")
    core = d % 2
    cx = (d // 2) % NX
    cy = d // (2 * NX)
    chip = d // 2
    side = cy // 2
    duo = ((cy + 1) // 2) % 2
    oy = NY - 1 - cy
    iy = cy + 1 - 2 * (cy % 2)
    me = side * 2 + core
    pal = chip * 2 + 1 - core
    outer = (oy * NX + cx) * 2 + core
    inner = (iy * NX + cx) * 2 + core
    right = (cy * NX + (cx + 1) % NX) * 2 + core
    left = (cy * NX + (cx + NX - 1) % NX) * 2 + core
    rows = w_hbm.shape[1]
    cols = w_hbm.shape[2]
    quarter = cols // 4
    per = g_hbm.shape[1]
    tokens = x_hbm.shape[1]
    band = tokens // NY

    def send(src, dst, s_sem, r_sem, zz, dd):
        pltpu.make_async_remote_copy(
            src_ref=src,
            dst_ref=dst,
            send_sem=s_sem,
            recv_sem=r_sem,
            device_id=(zz, dd),
            device_id_type=pl.DeviceIdType.MESH,
        ).start()

    def arrived(ref, sem):
        pltpu.make_async_copy(ref, ref, sem).wait()

    def column(i):
        off = (i % 2) * ((i + 1) // 2) + (1 - i % 2) * (NZ - i // 2)
        return (z + off) % NZ

    g_load = pltpu.make_async_copy(g_hbm, g_in, in_sem.at[1])
    x_load = pltpu.make_async_copy(x_hbm, x_in, in_sem.at[0])
    w_load = pltpu.make_async_copy(w_hbm.at[0], w.at[0], in_sem.at[2])
    m_load = pltpu.make_async_copy(m_hbm.at[0], m.at[0], in_sem.at[3])
    t_load = pltpu.make_async_copy(t_hbm.at[0], table.at[0], in_sem.at[4])
    own_load = pltpu.make_async_copy(
        bg_hbm.at[0, 0, pl.ds(2 * d, 2)], got.at[pl.ds(2 * d, 2)], in_sem.at[5]
    )
    g_load.start()
    barrier = pltpu.get_barrier_semaphore()

    @pl.loop(1, ND)
    def _(p):
        pl.semaphore_signal(
            barrier, inc=1, device_id=(z, (d + p) % ND), device_id_type=pl.DeviceIdType.MESH
        )

    @pl.loop(1, NZ)
    def _(p):
        for cc in range(2):
            pl.semaphore_signal(
                barrier,
                inc=1,
                device_id=((z + p) % NZ, chip * 2 + cc),
                device_id_type=pl.DeviceIdType.MESH,
            )

    x_load.start()
    w_load.start()
    m_load.start()
    t_load.start()
    own_load.start()

    def layer_of(s):
        found = jnp.int32(0)
        for l in range(NZ):
            found = jnp.where(owner[l] == s, l, found)
        return found
    g_load.wait()

    @pl.loop(0, NZ)
    def _(s):
        l = layer_of(s)
        for q in range(4):
            g_slot[s, q] = g_in[l, :, q * quarter : (q + 1) * quarter]

    g_all[z, duo, side, cx, pl.ds(core * per, per), :] = g_slot[z, me]
    pl.semaphore_wait(barrier, ND - 1 + 2 * (NZ - 1))
    def g_home(zs):
        return g_all.at[zs, duo, side, cx, pl.ds(core * per, per)]

    far = (z + NZ // 2) % NZ
    ways = (1, NZ - 1)
    deep = tokens // 2
    there = (1 - side) * 2 + core
    mine = pl.ds(2 * side, 2)
    theirs = pl.ds(2 * (1 - side), 2)

    def g_there(zs):
        return g_all.at[zs, duo, 1 - side, cx, pl.ds(core * per, per)]

    send(g_slot.at[z, side * 2 + 1 - core], g_home(z), go_send.at[0], gz_recv.at[z], z, pal)
    for cc in range(2):
        send(
            g_slot.at[z, (1 - side) * 2 + cc],
            g_home(z),
            go_send.at[1 + cc],
            gz_recv.at[z],
            z,
            (oy * NX + cx) * 2 + cc,
        )

    def g_cross(zt):
        send(g_slot.at[zt, theirs], g_other.at[zt], gx_send, gx_recv.at[zt], z, outer)

    g_cross((z + 1) % NZ)
    g_cross((z + NZ - 1) % NZ)
    g_cross(far)
    for j in (2, 3):
        g_cross((z + j) % NZ)
        g_cross((z + NZ - j) % NZ)

    send(g_slot.at[far, mine], g_relay.at[0], gr_send, gr_recv.at[0], (z + 1) % NZ, d)
    def g_own(j):
        for zt in ((z + j) % NZ, (z + NZ - j) % NZ):
            for cc in range(2):
                send(
                    g_slot.at[zt, 2 * side + cc],
                    g_home(z),
                    gz_send,
                    gz_recv.at[z],
                    zt,
                    chip * 2 + cc,
                )

    def g_for_other(j):
        for zt in ((z + j) % NZ, (z + NZ - j) % NZ):
            arrived(g_other.at[zt], gx_recv.at[zt])
            for cc in range(2):
                send(
                    g_other.at[zt, cc], g_there(z), gz_send, gz_recv.at[z], zt, chip * 2 + cc
                )

    def x_out(j):
        for h in range(2):
            for zt in ((z + j) % NZ, (z + NZ - j) % NZ):
                at = pl.ds(h * deep, deep)
                send(
                    x_slot.at[zt, at], x_all.at[z, me, at], xz_send, xz_recv.at[z, h], zt, d
                )

    def x_half(zs, s, h):
        return x_all.at[zs, s, pl.ds(pl.multiple_of(h * deep, deep), deep)]

    def x_share(zs, h):
        ref = x_half(zs, me, h)
        send(ref, ref, xo_send, xo_recv.at[zs, h], z, outer)
        send(ref, ref, xp_send, xp_recv.at[zs, h], z, pal)

    def x_first(j, h):
        for zs in ((z + j) % NZ, (z + NZ - j) % NZ):
            arrived(x_half(zs, me, h), xz_recv.at[zs, h])
            x_share(zs, h)

    def x_first_far(h):
        arrived(x_half(far, me, h), xz_recv.at[far, h])
        x_share(far, h)

    def x_second(zs, h):
        ref = x_half(zs, there, h)
        arrived(ref, xo_recv.at[zs, h])
        send(ref, ref, xp_send, xp_recv.at[zs, h], z, pal)

    def x_second_both(j, h):
        for zs in ((z + j) % NZ, (z + NZ - j) % NZ):
            x_second(zs, h)

    g_own(1)
    g_own(2)

    x_load.wait()

    @pl.loop(0, NZ)
    def _(s):
        l = layer_of(s)
        x_slot[s] = x_in[l]

    x_all[z, me] = x_slot[z]

    for way in range(2):
        for h in range(2):
            send(
                x_slot.at[far, pl.ds((2 * h + way) * band, band)],
                x_relay.at[way, h],
                xr_send,
                xr_recv.at[way, h],
                (z + ways[way]) % NZ,
                d,
            )

    for h in range(2):
        x_share(z, h)

    def whole(zs, pr, da):
        return g_all.at[zs, pr, :, (cx + da + NX) % NX]

    def part(zs, pr, da, h):
        return g_all.at[zs, pr, h, (cx + da + NX) % NX]

    def push(ref, zs, k, dd):
        send(ref, ref, ag_send, ag_recv.at[zs, k], z, dd)

    def landed(it):
        zs = column(it)

        @pl.when(it == 0)
        def _():
            arrived(g_slot.at[0, 0:3], gz_recv.at[zs])

        @pl.when(it > 0)
        def _():
            arrived(g_slot.at[0], gz_recv.at[zs])

    def feed(it):
        @pl.when(it == 0)
        def _():
            g_for_other(1)
            x_out(1)
            arrived(g_other.at[far], gx_recv.at[far])
            send(g_other.at[far], g_relay.at[1], gr_send, gr_recv.at[1], (z + NZ - 1) % NZ, d)

        @pl.when(it == 1)
        def _():
            g_for_other(2)
            g_own(3)
            g_for_other(3)
            x_out(2)

        @pl.when(it == 2)
        def _():
            relay()

    def relay():
        for way in range(2):
            zs = (z + NZ - ways[way]) % NZ
            zt = (zs + NZ // 2) % NZ
            arrived(g_relay.at[way], gr_recv.at[way])
            home = g_home(zs) if way == 0 else g_there(zs)
            sem = gz_recv.at[zs]
            for cc in range(2):
                send(g_relay.at[way, cc], home, gf_send, sem, zt, chip * 2 + cc)

        x_out(3)
        for way in range(2):
            zs = (z + NZ - ways[way]) % NZ
            zt = (zs + NZ // 2) % NZ
            for h in range(2):
                arrived(x_relay.at[way, h], xr_recv.at[way, h])
                send(
                    x_relay.at[way, h],
                    x_all.at[zs, me, pl.ds((2 * h + way) * band, band)],
                    xf_send,
                    xz_recv.at[zs, h],
                    zt,
                    d,
                )

    def multiply(u):
        k = u // 2
        h = u % 2
        zs = column(k)
        arrived(x_slot.at[0], xp_recv.at[zs, h])
        @pl.loop(0, 4)
        def _(s):
            for pr in range(2):
                y = pr + h * (NY - 1 - 2 * pr)
                x_turn[pl.ds(s * rows, rows), pr * band : (pr + 1) * band] = x_all[
                    zs, s, pl.ds(pl.multiple_of(y * band, band), band), :
                ].T

        @pl.loop(0, quarter // 256)
        def _(n):
            where = pl.ds(pl.multiple_of(n * 256, 256), 256)
            block = g_all[zs, :, h, :, :, where].reshape(deep, 256)
            acc[:, where] += jnp.dot(x_turn[...], block, preferred_element_type=jnp.float32)

    def x_stages(it):
        @pl.when(it == 2)
        def _():
            for h in range(2):
                x_second(z, h)

        def event(steps, do):
            for when, *what in steps:

                @pl.when(it == when)
                def _():
                    do(*what)

        event(
            ((3, 1, 0), (4, 1, 1), (5, 2, 0), (6, 2, 1), (8, 3, 0), (9, 3, 1)),
            x_first,
        )
        event(
            ((5, 1, 0), (6, 1, 1), (7, 2, 0), (8, 2, 1), (10, 3, 0), (11, 3, 1)),
            x_second_both,
        )
        event(((10, 0), (10, 1)), x_first_far)
        event(((12, far, 0), (13, far, 1)), x_second)

        first = jnp.where(
            it < 7, 0, jnp.where(it < 12, 2 * it - 12, it + 1)
        )
        count = jnp.where(
            it == 11, 3, jnp.where(it == 12, 1, jnp.where((it == 4) | (it >= 7), 2, 0))
        )

        @pl.loop(first, first + count)
        def _(v):
            multiply(v + jnp.where(v == 11, 1, 0) - jnp.where(v == 12, 1, 0))
    @pl.loop(0, ND)
    def _(j):
        for r in range(2):
            t = jnp.where(r < counts[0, 0, j], ids[0, 0, 2 * j + r], -1)
            tag[j, r : r + 1, :] = jnp.full((1, tag.shape[2]), t, jnp.int32)

    got_tag[d] = tag[d]
    acc[...] = jnp.zeros_like(acc)
    w_load.wait()

    def weight_step(i, total):
        v = w[0, pl.ds(pl.multiple_of(i * 8, 8), 8), :]
        v = v * v
        for k in range(cols // 128):
            total = total + v[:, k * 128 : (k + 1) * 128]
        return total

    weight_sq = lax.fori_loop(0, rows // 8, weight_step, jnp.zeros((8, 128), jnp.float32))
    @pl.when(core == 0)
    def _():
        @pl.loop(0, NZ + 6)
        def _(it):
            @pl.when(it < NZ)
            def _():
                zs = column(it)
                landed(it)
                push(whole(zs, duo, 0), zs, 0, right)
                push(whole(zs, duo, 0), zs, 1, left)
                push(whole(zs, duo, 0), zs, 3, inner)

            @pl.when((it >= 1) & (it < NZ + 1))
            def _():
                zs = column(it - 1)
                arrived(whole(zs, duo, -1), ag_recv.at[zs, 0])
                push(part(zs, duo, -1, 0), zs, 2, right)
                push(whole(zs, duo, -1), zs, 3, inner)
                arrived(whole(zs, duo, 1), ag_recv.at[zs, 1])
                push(part(zs, duo, 1, 1), zs, 2, left)
                push(whole(zs, duo, 1), zs, 3, inner)

            feed(it)

            @pl.when((it >= 2) & (it < NZ + 2))
            def _():
                zs = column(it - 2)
                arrived(whole(zs, duo, 2), ag_recv.at[zs, 2])
                push(whole(zs, duo, 2), zs, 3, inner)

            @pl.when((it >= 3) & (it < NZ + 3))
            def _():
                zs = column(it - 3)
                arrived(g_all.at[zs, 1 - duo], ag_recv.at[zs, 3])

            x_stages(it)

    @pl.when(core == 1)
    def _():
        @pl.loop(0, NZ + 6)
        def _(it):
            @pl.when(it < NZ)
            def _():
                zs = column(it)
                landed(it)
                push(whole(zs, duo, 0), zs, 3, inner)
                push(whole(zs, duo, 0), zs, 0, right)
                push(whole(zs, duo, 0), zs, 1, left)

            @pl.when((it >= 1) & (it < NZ + 1))
            def _():
                zs = column(it - 1)
                arrived(whole(zs, 1 - duo, 0), ag_recv.at[zs, 3])
                push(whole(zs, 1 - duo, 0), zs, 4, right)
                push(whole(zs, 1 - duo, 0), zs, 5, left)
                arrived(whole(zs, duo, -1), ag_recv.at[zs, 0])
                push(part(zs, duo, -1, 0), zs, 2, right)
                arrived(whole(zs, duo, 1), ag_recv.at[zs, 1])
                push(part(zs, duo, 1, 1), zs, 2, left)

            feed(it)

            @pl.when((it >= 2) & (it < NZ + 2))
            def _():
                zs = column(it - 2)
                arrived(whole(zs, 1 - duo, -1), ag_recv.at[zs, 4])
                push(part(zs, 1 - duo, -1, 0), zs, 6, right)
                arrived(whole(zs, 1 - duo, 1), ag_recv.at[zs, 5])
                push(part(zs, 1 - duo, 1, 1), zs, 6, left)
                arrived(whole(zs, duo, 2), ag_recv.at[zs, 2])

            @pl.when((it >= 3) & (it < NZ + 3))
            def _():
                zs = column(it - 3)
                arrived(whole(zs, 1 - duo, 2), ag_recv.at[zs, 6])

            x_stages(it)
    def grad_step(i, total):
        for k in range(4):
            v = acc[pl.ds(pl.multiple_of(i * 32 + k * 8, 8), 8), :]
            total = total + v * v
        return total

    wide_sq = lax.fori_loop(0, 4 * rows // 32, grad_step, jnp.zeros((8, quarter), jnp.float32))
    grad_sq = wide_sq[:, 0:128]
    for k in range(1, quarter // 128):
        grad_sq = grad_sq + wide_sq[:, k * 128 : (k + 1) * 128]
    norms[d, 0:1] = jnp.sum(weight_sq, axis=0, keepdims=True)
    norms[d, 1:2] = jnp.sum(grad_sq, axis=0, keepdims=True)
    grad[:, pl.ds(pl.multiple_of(me * quarter, quarter), quarter)] = acc[pl.ds(me * rows, rows), :]

    @pl.loop(1, ND)
    def _(p):
        send(norms.at[d], norms.at[d], norm_send, norm_recv, z, (d + p) % ND)
    mates = (
        (me, d),
        (side * 2 + 1 - core, pal),
        ((1 - side) * 2 + core, outer),
        ((1 - side) * 2 + 1 - core, outer + 1 - 2 * core),
    )

    def columns(k):
        return pl.ds(pl.multiple_of(mates[k][0] * quarter, quarter), quarter)

    for k in range(1, 4):
        send(
            acc.at[pl.ds(mates[k][0] * rows, rows)],
            grad.at[:, columns(0)],
            half_send,
            half_recv.at[k - 1],
            z,
            mates[k][1],
        )

    def block_out(j):
        send(tag.at[j], got_tag.at[d], tag_send, tag_recv, z, j)
        send(
            bg_hbm.at[0, 0, pl.ds(2 * j, 2)],
            got.at[pl.ds(2 * d, 2)],
            bg_send,
            bg_recv,
            z,
            j,
        )

    near = ND // 2
    m_load.wait()

    arrived(norms.at[0 : ND - 1], norm_recv)
    totals = jnp.sum(norms[...], axis=0)
    weight_total = jnp.sum(totals[0:1], keepdims=True)
    grad_total = jnp.sum(totals[1:2], keepdims=True)
    weight_norm = jnp.sqrt(weight_total + eps_norm)
    trust = weight_norm / (jnp.sqrt(grad_total + eps_norm) + tower_decay * weight_norm)
    scale = tower_rate * trust

    strip = 16
    up = (z + 1) % NZ
    down = (z + NZ - 1) % NZ

    def piece(s, k):
        return slabs.at[s, mates[k][0]]

    def renew(k):
        @pl.loop(0, rows // strip)
        def _(i):
            at = pl.ds(pl.multiple_of(i * strip, strip), strip)
            old = w[0, at, columns(k)]
            new_m = momentum_keep * m[0, at, columns(k)] + scale * (
                grad[at, columns(k)] + tower_decay * old
            )
            new_w = old - new_m
            m[0, at, columns(k)] = new_m
            w[0, at, columns(k)] = new_w
            slabs[z, mates[k][0], at, :] = new_w.astype(jnp.bfloat16)

        send(piece(z, k), piece(z, k), wz_send, wz_recv.at[0, 0, k], up, d)
        send(piece(z, k), piece(z, k), wz_send, wz_recv.at[1, 0, k], down, d)

    def onward(j, ks):
        low = (z + NZ - j) % NZ
        high = (z + j) % NZ
        for k in ks:
            if j < 3 or k % 2 == 0:
                arrived(piece(low, k), wz_recv.at[0, j - 1, k])
                send(piece(low, k), piece(low, k), wz_send, wz_recv.at[0, j, k], up, d)
            if j < 3 or k % 2 == 1:
                arrived(piece(high, k), wz_recv.at[1, j - 1, k])
                send(piece(high, k), piece(high, k), wz_send, wz_recv.at[1, j, k], down, d)
    renew(0)
    arrived(grad.at[:, columns(1)], half_recv.at[0])
    renew(1)

    @pl.loop(1, near)
    def _(p):
        block_out(side * near + (d + p) % near)
    onward(1, (0,))
    arrived(grad.at[:, columns(2)], half_recv.at[1])
    renew(2)
    onward(1, (1,))
    onward(2, (0,))
    arrived(grad.at[:, columns(3)], half_recv.at[2])
    renew(3)
    @pl.loop(0, near)
    def _(p):
        block_out((1 - side) * near + (d + p) % near)
    onward(2, (1,))
    onward(1, (2, 3))
    onward(3, (0, 1))
    onward(2, (2, 3))
    onward(3, (2, 3))
    own_load.wait()
    t_load.wait()

    arrived(got.at[0 : 2 * (ND - 1)], bg_recv)
    arrived(got_tag.at[0 : ND - 1], tag_recv)
    nb = table.shape[1]
    wide = table.shape[3]
    lane = lax.broadcasted_iota(jnp.int32, (strip, wide), 1)
    same = lane % strip == lax.broadcasted_iota(jnp.int32, (strip, wide), 0)
    names = lane // strip

    @pl.loop(0, ND)
    def _(s):
        for r in range(2):
            hit = (got_tag[s, r : r + 1, :] == names) & same
            pick[2 * s + r] = jnp.where(hit, 1.0, 0.0).astype(jnp.bfloat16)

    turned[...] = pick[...].reshape(2 * ND * strip, wide).T

    @pl.loop(0, table.shape[2] // strip)
    def _(i):
        at = pl.ds(pl.multiple_of(i * strip, strip), strip)
        values = got[:, at, :].reshape(2 * ND * strip, wide)
        total = jnp.dot(turned[...], values, preferred_element_type=jnp.float32)
        sums[:, at, :] = total.reshape(nb, strip, wide)

    tags = got_tag[:, 0:2, :]
    for b in range(nb):
        hits = jnp.sum(jnp.where(tags == b, 1.0, 0.0), axis=(0, 1)).reshape(1, wide)
        flat = table[0, b]
        total = sums[b]
        w_norm = jnp.sqrt(jnp.sum(flat * flat, keepdims=True) + eps_norm)
        g_norm = jnp.sqrt(jnp.sum(total * total, keepdims=True) + eps_norm)
        block_trust = w_norm / (g_norm + table_decay * w_norm)
        moved = flat - table_rate * block_trust * (total + table_decay * flat)
        table[0, b] = jnp.where(hits > 0, moved, flat)
    low = (z + NZ - 3) % NZ
    high = (z + 3) % NZ
    for k in range(4):
        if k % 2 == 0:
            arrived(piece(high, k), wz_recv.at[1, 2, k])
            arrived(piece(far, k), wz_recv.at[0, 3, k])
        else:
            arrived(piece(low, k), wz_recv.at[0, 2, k])
            arrived(piece(far, k), wz_recv.at[1, 3, k])
    arrived(g_slot.at[0:6], gz_send)
    for k in range(3):
        arrived(g_slot.at[0, 0], go_send.at[k])
    arrived(g_other.at[0:7], gx_send)
    arrived(g_relay, gr_send)
    arrived(g_relay, gf_send)
    arrived(x_slot.at[0:6], xz_send)
    arrived(x_relay, xr_send)
    arrived(x_relay, xf_send)
    arrived(x_all.at[:, 0], xo_send)
    arrived(x_all.at[:, 0:2], xp_send)
    arrived(g_all.at[0:7], ag_send)
    arrived(acc.at[0 : 3 * rows], half_send)
    arrived(norms.at[0 : ND - 1], norm_send)
    arrived(got.at[0 : 2 * (ND - 1)], bg_send)
    arrived(tag.at[0 : ND - 1], tag_send)
    arrived(slabs.at[0:7], wz_send)


def finish_kernel(owner, slots, new_w, new_m, new_t, out, w_out, m_out, t_out, sem):
    copies = [
        pltpu.make_async_copy(
            slots.at[owner[l], q],
            out.at[l, :, q * slots.shape[3] : (q + 1) * slots.shape[3]],
            sem.at[4 * l + q],
        )
        for l in range(NZ)
        for q in range(4)
    ] + [
        pltpu.make_async_copy(new_w, w_out, sem.at[4 * NZ]),
        pltpu.make_async_copy(new_m, m_out, sem.at[4 * NZ + 1]),
        pltpu.make_async_copy(new_t, t_out, sem.at[4 * NZ + 2]),
    ]
    for copy in copies:
        copy.start()
    for copy in copies:
        copy.wait()


def local(
    layer_inputs,
    output_grads,
    layer_owner,
    master_weights,
    momentum,
    table_blocks,
    block_grads,
    block_ids,
    block_counts,
):
    layers, tokens, rows = layer_inputs.shape
    per, cols = output_grads.shape[1:]
    quarter = cols // 4
    nb, tall, wide = table_blocks.shape[1:]
    f32, bf16, i32 = jnp.float32, jnp.bfloat16, jnp.int32
    hbm = pl.BlockSpec(memory_space=pltpu.HBM)
    smem = pl.BlockSpec(memory_space=pltpu.SMEM)
    anywhere = pl.BlockSpec(memory_space=pl.ANY)
    dma = pltpu.SemaphoreType.DMA
    slots, new_w, new_m, new_t = pl.pallas_call(
        step_kernel,
        name="step",
        out_shape=(
            pltpu.VMEM((NZ, 4, rows, quarter), bf16),
            pltpu.VMEM(master_weights.shape, f32),
            pltpu.VMEM(momentum.shape, f32),
            pltpu.VMEM(table_blocks.shape, f32),
        ),
        in_specs=[smem, smem, smem] + [hbm] * 6,
        out_specs=(pl.BlockSpec(memory_space=pltpu.VMEM),) * 4,
        scratch_shapes=[
            pltpu.VMEM((layers, tokens, rows), bf16),
            pltpu.VMEM((layers, tokens, rows), bf16),
            pltpu.VMEM((NZ, 4, tokens, rows), bf16),
            pltpu.VMEM((4 * rows, tokens // 2), bf16),
            pltpu.VMEM((2, 2, tokens // NY, rows), bf16),
            pltpu.VMEM((layers, per, cols), bf16),
            pltpu.VMEM((layers, 4, per, quarter), bf16),
            pltpu.VMEM((layers, 2, per, quarter), bf16),
            pltpu.VMEM((NZ, 2, 2, NX, 2 * per, quarter), bf16),
            pltpu.VMEM((2, 2, per, quarter), bf16),
            pltpu.VMEM((4 * rows, quarter), f32),
            pltpu.VMEM((rows, cols), f32),
            pltpu.VMEM((nb, tall, wide), f32),
            pltpu.VMEM((2 * ND, wide // nb, wide), bf16),
            pltpu.VMEM((wide, 2 * ND * (wide // nb)), bf16),
            pltpu.VMEM((2 * ND, tall, wide), bf16),
            pltpu.VMEM((ND, 8, wide), i32),
            pltpu.VMEM((ND, 8, wide), i32),
            pltpu.VMEM((ND, 2, 128), f32),
            dma((6,)),
            dma,
            dma((NZ,)),
            dma((3,)),
            dma,
            dma((NZ,)),
            dma,
            dma((2,)),
            dma,
            dma,
            dma((NZ, 2)),
            dma,
            dma((2, 2)),
            dma,
            dma,
            dma((NZ, 2)),
            dma,
            dma((NZ, 2)),
            dma,
            dma((NZ, 7)),
            dma,
            dma((3,)),
            dma,
            dma,
            dma,
            dma,
            dma,
            dma,
            dma,
            dma((2, 4, 4)),
        ],
        compiler_params=pltpu.CompilerParams(
            collective_id=0, has_side_effects=True, vmem_limit_bytes=60_160_000
        ),
    )(
        layer_owner,
        block_ids,
        block_counts,
        layer_inputs,
        output_grads,
        master_weights,
        momentum,
        table_blocks,
        block_grads,
    )
    new_weights, new_master, new_moment, new_table = pl.pallas_call(
        finish_kernel,
        name="finish",
        in_specs=[smem] + [anywhere] * 4,
        out_specs=(hbm,) * 4,
        scratch_shapes=[dma((4 * NZ + 3,))],
        out_shape=(
            jax.ShapeDtypeStruct((layers, rows, cols), bf16),
            jax.ShapeDtypeStruct(master_weights.shape, f32),
            jax.ShapeDtypeStruct(momentum.shape, f32),
            jax.ShapeDtypeStruct(table_blocks.shape, f32),
        ),
        compiler_params=pltpu.CompilerParams(vmem_limit_bytes=1024 * 1024),
    )(layer_owner, slots, new_w, new_m, new_t)
    return new_master, new_moment, new_weights, new_table


def solution(mesh):
    return jax.shard_map(
        local,
        mesh=mesh,
        in_specs=(
            P(None, "grp", "dev"),
            P(None, ("grp", "dev"), None),
            P(),
            P("grp", "dev", None),
            P("grp", "dev", None),
            P("grp", "dev", None, None),
            P("grp", "dev", None, None, None),
            P("grp", "dev", None),
            P("grp", "dev", None),
        ),
        out_specs=(
            P("grp", "dev", None),
            P("grp", "dev", None),
            P(None, "dev", None),
            P("grp", "dev", None, None),
        ),
        check_vma=False,
    )
```

time: 154 us -> 147 us (0.955)
  Pallas kernels: 153 us -> 146 us
    pallas_call x1, Pallas kernels: 149 us -> 142 us  [local(): pl.pallas_call(step_kernel, name='step', out_shape=(pltpu.VMEM((NZ, 4, ro...]
where the time goes in v2:
time: 147 us; the launch traced here: 146 us
  Pallas kernels  146 us (99%)
    pallas_call x1, Pallas kernels, local(): pl.pallas_call(step_kernel, name='step', out_shape=(pltpu.VMEM((NZ, 4, ro...  142 us
    pallas_call x1, Pallas kernels, local(): pl.pallas_call(finish_kernel, name='finish', in_specs=[smem] + [anywhere]...  3.65 us

profile of v2, /device:TPU:1, one launch (start us, length us, event | category | flops | bytes accessed | tf_op | source)
XLA Modules:
  0.0 146.5 jit_solution(3476177886317840291)
XLA Ops:
  0.6 0.0 copy-start
  0.6 142.2 %step.1 = (bf16[8,4,128,512]{3,2,1,0:T(8,128)(2,1)S(1)}, f32[1,128,2048]{2,1,0:T(8,128)S(1)}, f32[1,128,2048]{2,1,0:T(8,128)S(1)}, f32[1,8,128,128]{3,2,1,0:T(8,128)S(1)}) custom-call(s32[8]{0:T(128)} %owner.3, s32[1,1,64]{2,1,0:T(1,128)} %ids.1, s32[1,1,32]{2,1,0:T(1,128)} %counts.1, bf16[8,1024,128]{2,1,0:T(8,128)(2,1)} %x_hbm.1, ...), custom_call_target="tpu_custom_call" | custom-call | tf_op jit(solution)/shard_map/step/pallas_call | solution.py:720
  142.8 0.0 copy-done
  142.8 3.6 %finish.1 = (bf16[8,128,2048]{2,1,0:T(8,128)(2,1)}, f32[1,128,2048]{2,1,0:T(8,128)}, f32[1,128,2048]{2,1,0:T(8,128)}, f32[1,8,128,128]{3,2,1,0:T(8,128)}) custom-call(s32[8]{0:T(128)S(1)} %copy-done, bf16[8,4,128,512]{3,2,1,0:T(8,128)(2,1)S(1)} %get-tuple-element.12.slots, f32[1,128,2048]{2,1,0:T(8,128)S(1)} %get-tuple-element.13.new_w, ...), custom_call_target="tpu_custom_call" | custom-call | tf_op jit(solution)/shard_map/finish/pallas_call | solution.py:796
Async XLA Ops:
  0.6 142.2 %copy-start = (s32[8]{0:T(128)S(1)}, s32[8]{0:T(128)}, u32[]{:S(2)}) copy-start(s32[8]{0:T(128)} %owner.3) | copy-start | bytes 100

commit v3 on v2

--- a/solution.py
+++ b/solution.py
@@ -37,7 +37,6 @@
     x_in,
     x_slot,
     x_all,
-    x_turn,
     x_relay,
     g_in,
     g_slot,
@@ -177,7 +176,6 @@
 
     far = (z + NZ // 2) % NZ
     ways = (1, NZ - 1)
-    deep = tokens // 2
     there = (1 - side) * 2 + core
     mine = pl.ds(2 * side, 2)
     theirs = pl.ds(2 * (1 - side), 2)
@@ -230,13 +228,13 @@
     def x_out(j):
         for h in range(2):
             for zt in ((z + j) % NZ, (z + NZ - j) % NZ):
-                at = pl.ds(h * deep, deep)
+                at = pl.ds(2 * h, 2)
                 send(
                     x_slot.at[zt, at], x_all.at[z, me, at], xz_send, xz_recv.at[z, h], zt, d
                 )
 
     def x_half(zs, s, h):
-        return x_all.at[zs, s, pl.ds(pl.multiple_of(h * deep, deep), deep)]
+        return x_all.at[zs, s, pl.ds(2 * h, 2)]
 
     def x_share(zs, h):
         ref = x_half(zs, me, h)
@@ -269,14 +267,15 @@
     @pl.loop(0, NZ)
     def _(s):
         l = layer_of(s)
-        x_slot[s] = x_in[l]
+        for y in range(NY):
+            x_slot[s, y] = x_in[l, y * band : (y + 1) * band, :].T
 
     x_all[z, me] = x_slot[z]
 
     for way in range(2):
         for h in range(2):
             send(
-                x_slot.at[far, pl.ds((2 * h + way) * band, band)],
+                x_slot.at[far, 2 * h + way],
                 x_relay.at[way, h],
                 xr_send,
                 xr_recv.at[way, h],
@@ -344,7 +343,7 @@
                 arrived(x_relay.at[way, h], xr_recv.at[way, h])
                 send(
                     x_relay.at[way, h],
-                    x_all.at[zs, me, pl.ds((2 * h + way) * band, band)],
+                    x_all.at[zs, me, 2 * h + way],
                     xf_send,
                     xz_recv.at[zs, h],
                     zt,
@@ -356,19 +355,18 @@
         h = u % 2
         zs = column(k)
         arrived(x_slot.at[0], xp_recv.at[zs, h])
-        @pl.loop(0, 4)
-        def _(s):
-            for pr in range(2):
-                y = pr + h * (NY - 1 - 2 * pr)
-                x_turn[pl.ds(s * rows, rows), pr * band : (pr + 1) * band] = x_all[
-                    zs, s, pl.ds(pl.multiple_of(y * band, band), band), :
-                ].T
-
         @pl.loop(0, quarter // 256)
         def _(n):
             where = pl.ds(pl.multiple_of(n * 256, 256), 256)
-            block = g_all[zs, :, h, :, :, where].reshape(deep, 256)
-            acc[:, where] += jnp.dot(x_turn[...], block, preferred_element_type=jnp.float32)
+            total = acc[:, where]
+            for pr in range(2):
+                y = pr + h * (NY - 1 - 2 * pr)
+                total = total + jnp.dot(
+                    x_all[zs, :, y].reshape(4 * rows, band),
+                    g_all[zs, pr, h, :, :, where].reshape(band, 256),
+                    preferred_element_type=jnp.float32,
+                )
+            acc[:, where] = total
 
     def x_stages(it):
         @pl.when(it == 2)
@@ -562,35 +560,50 @@
     up = (z + 1) % NZ
     down = (z + NZ - 1) % NZ
 
-    def piece(s, k):
-        return slabs.at[s, mates[k][0]]
+    cut = rows // 2
+
+    def piece(s, k, r):
+        return slabs.at[s, mates[k][0], pl.ds(r * cut, cut)]
+
+    def pass_on(s, k, r, way, hop):
+        send(
+            piece(s, k, r),
+            piece(s, k, r),
+            wz_send,
+            wz_recv.at[way, hop, 2 * k + r],
+            (up, down)[way],
+            d,
+        )
+
+    def came(s, k, r, way, hop):
+        arrived(piece(s, k, r), wz_recv.at[way, hop, 2 * k + r])
 
     def renew(k):
-        @pl.loop(0, rows // strip)
-        def _(i):
-            at = pl.ds(pl.multiple_of(i * strip, strip), strip)
-            old = w[0, at, columns(k)]
-            new_m = momentum_keep * m[0, at, columns(k)] + scale * (
-                grad[at, columns(k)] + tower_decay * old
-            )
-            new_w = old - new_m
-            m[0, at, columns(k)] = new_m
-            w[0, at, columns(k)] = new_w
-            slabs[z, mates[k][0], at, :] = new_w.astype(jnp.bfloat16)
-
-        send(piece(z, k), piece(z, k), wz_send, wz_recv.at[0, 0, k], up, d)
-        send(piece(z, k), piece(z, k), wz_send, wz_recv.at[1, 0, k], down, d)
+        for r in range(2):
+
+            @pl.loop(0, cut // strip)
+            def _(i):
+                at = pl.ds(pl.multiple_of(r * cut + i * strip, strip), strip)
+                old = w[0, at, columns(k)]
+                new_m = momentum_keep * m[0, at, columns(k)] + scale * (
+                    grad[at, columns(k)] + tower_decay * old
+                )
+                new_w = old - new_m
+                m[0, at, columns(k)] = new_m
+                w[0, at, columns(k)] = new_w
+                slabs[z, mates[k][0], at, :] = new_w.astype(jnp.bfloat16)
+
+            for way in range(2):
+                pass_on(z, k, r, way, 0)
 
     def onward(j, ks):
-        low = (z + NZ - j) % NZ
-        high = (z + j) % NZ
         for k in ks:
-            if j < 3 or k % 2 == 0:
-                arrived(piece(low, k), wz_recv.at[0, j - 1, k])
-                send(piece(low, k), piece(low, k), wz_send, wz_recv.at[0, j, k], up, d)
-            if j < 3 or k % 2 == 1:
-                arrived(piece(high, k), wz_recv.at[1, j - 1, k])
-                send(piece(high, k), piece(high, k), wz_send, wz_recv.at[1, j, k], down, d)
+            for r in range(2):
+                for way in range(2):
+                    if j < 3 or k % 2 == way:
+                        s = ((z + NZ - j) % NZ, (z + j) % NZ)[way]
+                        came(s, k, r, way, j - 1)
+                        pass_on(s, k, r, way, j)
     renew(0)
     arrived(grad.at[:, columns(1)], half_recv.at[0])
     renew(1)
@@ -649,15 +662,11 @@
         block_trust = w_norm / (g_norm + table_decay * w_norm)
         moved = flat - table_rate * block_trust * (total + table_decay * flat)
         table[0, b] = jnp.where(hits > 0, moved, flat)
-    low = (z + NZ - 3) % NZ
-    high = (z + 3) % NZ
     for k in range(4):
-        if k % 2 == 0:
-            arrived(piece(high, k), wz_recv.at[1, 2, k])
-            arrived(piece(far, k), wz_recv.at[0, 3, k])
-        else:
-            arrived(piece(low, k), wz_recv.at[0, 2, k])
-            arrived(piece(far, k), wz_recv.at[1, 3, k])
+        way = k % 2
+        for r in range(2):
+            came(((z + 3) % NZ, (z + NZ - 3) % NZ)[way], k, r, 1 - way, 2)
+            came(far, k, r, way, 3)
     arrived(g_slot.at[0:6], gz_send)
     for k in range(3):
         arrived(g_slot.at[0, 0], go_send.at[k])
@@ -730,10 +739,9 @@
         out_specs=(pl.BlockSpec(memory_space=pltpu.VMEM),) * 4,
         scratch_shapes=[
             pltpu.VMEM((layers, tokens, rows), bf16),
-            pltpu.VMEM((layers, tokens, rows), bf16),
-            pltpu.VMEM((NZ, 4, tokens, rows), bf16),
-            pltpu.VMEM((4 * rows, tokens // 2), bf16),
-            pltpu.VMEM((2, 2, tokens // NY, rows), bf16),
+            pltpu.VMEM((layers, NY, rows, tokens // NY), bf16),
+            pltpu.VMEM((NZ, 4, NY, rows, tokens // NY), bf16),
+            pltpu.VMEM((2, 2, rows, tokens // NY), bf16),
             pltpu.VMEM((layers, per, cols), bf16),
             pltpu.VMEM((layers, 4, per, quarter), bf16),
             pltpu.VMEM((layers, 2, per, quarter), bf16),
@@ -777,7 +785,7 @@
             dma,
             dma,
             dma,
-            dma((2, 4, 4)),
+            dma((2, 4, 8)),
         ],
         compiler_params=pltpu.CompilerParams(
             collective_id=0, has_side_effects=True, vmem_limit_bytes=60_160_000

time: 147 us -> 145 us (0.986)
  Pallas kernels: 146 us -> 144 us
    pallas_call x1, Pallas kernels: 142 us -> 140 us  [local(): pl.pallas_call(step_kernel, name='step', out_shape=(pltpu.VMEM((NZ, 4, ro...]
where the time goes in v3:
time: 145 us
  Pallas kernels  144 us (99%)
    pallas_call x1, Pallas kernels, local(): pl.pallas_call(step_kernel, name='step', out_shape=(pltpu.VMEM((NZ, 4, ro...  140 us
    pallas_call x1, Pallas kernels, local(): pl.pallas_call(finish_kernel, name='finish', in_specs=[smem] + [anywhere]...  3.65 us

profile of v3, /device:TPU:1, one launch (start us, length us, event | category | flops | bytes accessed | tf_op | source)
XLA Modules:
  0.0 144.8 jit_solution(2170574984351659685)
XLA Ops:
  0.6 0.0 copy-start
  0.6 140.5 %step.1 = (bf16[8,4,128,512]{3,2,1,0:T(8,128)(2,1)S(1)}, f32[1,128,2048]{2,1,0:T(8,128)S(1)}, f32[1,128,2048]{2,1,0:T(8,128)S(1)}, f32[1,8,128,128]{3,2,1,0:T(8,128)S(1)}) custom-call(s32[8]{0:T(128)} %owner.3, s32[1,1,64]{2,1,0:T(1,128)} %ids.1, s32[1,1,32]{2,1,0:T(1,128)} %counts.1, bf16[8,1024,128]{2,1,0:T(8,128)(2,1)} %x_hbm.1, ...), custom_call_target="tpu_custom_call" | custom-call | tf_op jit(solution)/shard_map/step/pallas_call | solution.py:729
  141.1 0.0 copy-done
  141.1 3.6 %finish.1 = (bf16[8,128,2048]{2,1,0:T(8,128)(2,1)}, f32[1,128,2048]{2,1,0:T(8,128)}, f32[1,128,2048]{2,1,0:T(8,128)}, f32[1,8,128,128]{3,2,1,0:T(8,128)}) custom-call(s32[8]{0:T(128)S(1)} %copy-done, bf16[8,4,128,512]{3,2,1,0:T(8,128)(2,1)S(1)} %get-tuple-element.12.slots, f32[1,128,2048]{2,1,0:T(8,128)S(1)} %get-tuple-element.13.new_w, ...), custom_call_target="tpu_custom_call" | custom-call | tf_op jit(solution)/shard_map/finish/pallas_call | solution.py:804
Async XLA Ops:
  0.6 140.5 %copy-start = (s32[8]{0:T(128)S(1)}, s32[8]{0:T(128)}, u32[]{:S(2)}) copy-start(s32[8]{0:T(128)} %owner.3) | copy-start | bytes 100

commit v4 on v3

--- a/solution.py
+++ b/solution.py
@@ -21,9 +21,9 @@
 
 
 def step_kernel(
-    owner,
-    ids,
-    counts,
+    owner_hbm,
+    ids_hbm,
+    counts_hbm,
     x_hbm,
     g_hbm,
     w_hbm,
@@ -52,6 +52,10 @@
     tag,
     got_tag,
     norms,
+    grad_sq,
+    owner,
+    ids,
+    counts,
     in_sem,
     gz_send,
     gz_recv,
@@ -131,6 +135,10 @@
     own_load = pltpu.make_async_copy(
         bg_hbm.at[0, 0, pl.ds(2 * d, 2)], got.at[pl.ds(2 * d, 2)], in_sem.at[5]
     )
+    owner_load = pltpu.make_async_copy(owner_hbm, owner, in_sem.at[6])
+    ids_load = pltpu.make_async_copy(ids_hbm, ids, in_sem.at[7])
+    counts_load = pltpu.make_async_copy(counts_hbm, counts, in_sem.at[8])
+    owner_load.start()
     g_load.start()
     barrier = pltpu.get_barrier_semaphore()
 
@@ -155,12 +163,15 @@
     m_load.start()
     t_load.start()
     own_load.start()
+    ids_load.start()
+    counts_load.start()
 
     def layer_of(s):
         found = jnp.int32(0)
         for l in range(NZ):
             found = jnp.where(owner[l] == s, l, found)
         return found
+    owner_load.wait()
     g_load.wait()
 
     @pl.loop(0, NZ)
@@ -350,7 +361,7 @@
                     d,
                 )
 
-    def multiply(u):
+    def multiply(u, final=False):
         k = u // 2
         h = u % 2
         zs = column(k)
@@ -367,6 +378,9 @@
                     preferred_element_type=jnp.float32,
                 )
             acc[:, where] = total
+            if final:
+                squares = jnp.sum((total * total).reshape(4 * rows // 8, 8, 256), axis=0)
+                grad_sq[...] += squares[:, :128] + squares[:, 128:]
 
     def x_stages(it):
         @pl.when(it == 2)
@@ -396,12 +410,15 @@
             it < 7, 0, jnp.where(it < 12, 2 * it - 12, it + 1)
         )
         count = jnp.where(
-            it == 11, 3, jnp.where(it == 12, 1, jnp.where((it == 4) | (it >= 7), 2, 0))
+            it == 11, 3, jnp.where(it >= 12, 1, jnp.where((it == 4) | (it >= 7), 2, 0))
         )
 
         @pl.loop(first, first + count)
         def _(v):
             multiply(v + jnp.where(v == 11, 1, 0) - jnp.where(v == 12, 1, 0))
+    ids_load.wait()
+    counts_load.wait()
+
     @pl.loop(0, ND)
     def _(j):
         for r in range(2):
@@ -420,6 +437,8 @@
         return total
 
     weight_sq = lax.fori_loop(0, rows // 8, weight_step, jnp.zeros((8, 128), jnp.float32))
+    norms[d, 0:1] = jnp.sum(weight_sq, axis=0, keepdims=True)
+    grad_sq[...] = jnp.zeros_like(grad_sq)
     @pl.when(core == 0)
     def _():
         @pl.loop(0, NZ + 6)
@@ -497,18 +516,8 @@
                 arrived(whole(zs, 1 - duo, 2), ag_recv.at[zs, 6])
 
             x_stages(it)
-    def grad_step(i, total):
-        for k in range(4):
-            v = acc[pl.ds(pl.multiple_of(i * 32 + k * 8, 8), 8), :]
-            total = total + v * v
-        return total
-
-    wide_sq = lax.fori_loop(0, 4 * rows // 32, grad_step, jnp.zeros((8, quarter), jnp.float32))
-    grad_sq = wide_sq[:, 0:128]
-    for k in range(1, quarter // 128):
-        grad_sq = grad_sq + wide_sq[:, k * 128 : (k + 1) * 128]
-    norms[d, 0:1] = jnp.sum(weight_sq, axis=0, keepdims=True)
-    norms[d, 1:2] = jnp.sum(grad_sq, axis=0, keepdims=True)
+    multiply(2 * NZ - 1, final=True)
+    norms[d, 1:2] = jnp.sum(grad_sq[...], axis=0, keepdims=True)
     grad[:, pl.ds(pl.multiple_of(me * quarter, quarter), quarter)] = acc[pl.ds(me * rows, rows), :]
 
     @pl.loop(1, ND)
@@ -686,22 +695,29 @@
     arrived(slabs.at[0:7], wz_send)
 
 
-def finish_kernel(owner, slots, new_w, new_m, new_t, out, w_out, m_out, t_out, sem):
+def finish_kernel(
+    owner_hbm, slots, new_w, new_m, new_t, out, w_out, m_out, t_out, owner, sem, own_sem
+):
+    owner_load = pltpu.make_async_copy(owner_hbm, owner, own_sem)
+    owner_load.start()
     copies = [
-        pltpu.make_async_copy(
-            slots.at[owner[l], q],
-            out.at[l, :, q * slots.shape[3] : (q + 1) * slots.shape[3]],
-            sem.at[4 * l + q],
-        )
-        for l in range(NZ)
-        for q in range(4)
-    ] + [
         pltpu.make_async_copy(new_w, w_out, sem.at[4 * NZ]),
         pltpu.make_async_copy(new_m, m_out, sem.at[4 * NZ + 1]),
         pltpu.make_async_copy(new_t, t_out, sem.at[4 * NZ + 2]),
     ]
     for copy in copies:
         copy.start()
+    owner_load.wait()
+    wide = slots.shape[3]
+    for l in range(NZ):
+        for q in range(4):
+            copy = pltpu.make_async_copy(
+                slots.at[owner[l], q],
+                out.at[l, :, q * wide : (q + 1) * wide],
+                sem.at[4 * l + q],
+            )
+            copy.start()
+            copies.append(copy)
     for copy in copies:
         copy.wait()
 
@@ -723,7 +739,6 @@
     nb, tall, wide = table_blocks.shape[1:]
     f32, bf16, i32 = jnp.float32, jnp.bfloat16, jnp.int32
     hbm = pl.BlockSpec(memory_space=pltpu.HBM)
-    smem = pl.BlockSpec(memory_space=pltpu.SMEM)
     anywhere = pl.BlockSpec(memory_space=pl.ANY)
     dma = pltpu.SemaphoreType.DMA
     slots, new_w, new_m, new_t = pl.pallas_call(
@@ -735,7 +750,7 @@
             pltpu.VMEM(momentum.shape, f32),
             pltpu.VMEM(table_blocks.shape, f32),
         ),
-        in_specs=[smem, smem, smem] + [hbm] * 6,
+        in_specs=[hbm] * 9,
         out_specs=(pl.BlockSpec(memory_space=pltpu.VMEM),) * 4,
         scratch_shapes=[
             pltpu.VMEM((layers, tokens, rows), bf16),
@@ -756,7 +771,11 @@
             pltpu.VMEM((ND, 8, wide), i32),
             pltpu.VMEM((ND, 8, wide), i32),
             pltpu.VMEM((ND, 2, 128), f32),
-            dma((6,)),
+            pltpu.VMEM((8, 128), f32),
+            pltpu.SMEM(layer_owner.shape, i32),
+            pltpu.SMEM(block_ids.shape, i32),
+            pltpu.SMEM(block_counts.shape, i32),
+            dma((9,)),
             dma,
             dma((NZ,)),
             dma((3,)),
@@ -804,9 +823,9 @@
     new_weights, new_master, new_moment, new_table = pl.pallas_call(
         finish_kernel,
         name="finish",
-        in_specs=[smem] + [anywhere] * 4,
+        in_specs=[anywhere] * 5,
         out_specs=(hbm,) * 4,
-        scratch_shapes=[dma((4 * NZ + 3,))],
+        scratch_shapes=[pltpu.SMEM(layer_owner.shape, i32), dma((4 * NZ + 3,)), dma],
         out_shape=(
             jax.ShapeDtypeStruct((layers, rows, cols), bf16),
             jax.ShapeDtypeStruct(master_weights.shape, f32),

time: 145 us -> 143 us (0.986)
  no operation moved by 1% of the time
where the time goes in v4:
time: 143 us
  Pallas kernels  143 us (100%)
    pallas_call x1, Pallas kernels, local(): pl.pallas_call(step_kernel, name='step', out_shape=(pltpu.VMEM((NZ, 4, ro...  140 us
    pallas_call x1, Pallas kernels, local(): pl.pallas_call(finish_kernel, name='finish', in_specs=[anywhere] * 5, out...  3.09 us

profile of v4, /device:TPU:1, one launch (start us, length us, event | category | flops | bytes accessed | tf_op | source)
XLA Modules:
  0.0 143.3 jit_solution(15056072180447569773)
XLA Ops:
  0.6 0.0 copy-start
  0.6 139.5 %step.1 = (bf16[8,4,128,512]{3,2,1,0:T(8,128)(2,1)S(1)}, f32[1,128,2048]{2,1,0:T(8,128)S(1)}, f32[1,128,2048]{2,1,0:T(8,128)S(1)}, f32[1,8,128,128]{3,2,1,0:T(8,128)S(1)}) custom-call(s32[8]{0:T(128)} %owner_hbm.3, s32[1,1,64]{2,1,0:T(1,128)} %ids_hbm.1, s32[1,1,32]{2,1,0:T(1,128)} %counts_hbm.1, bf16[8,1024,128]{2,1,0:T(8,128)(2,1)} %x_hbm.1, ...), custom_call_target="tpu_custom_call" | custom-call | tf_op jit(solution)/shard_map/step/pallas_call | solution.py:744
  140.2 0.0 copy-done
  140.2 3.1 %finish.1 = (bf16[8,128,2048]{2,1,0:T(8,128)(2,1)}, f32[1,128,2048]{2,1,0:T(8,128)}, f32[1,128,2048]{2,1,0:T(8,128)}, f32[1,8,128,128]{3,2,1,0:T(8,128)}) custom-call(s32[8]{0:T(128)S(1)} %copy-done, bf16[8,4,128,512]{3,2,1,0:T(8,128)(2,1)S(1)} %get-tuple-element.12.slots, f32[1,128,2048]{2,1,0:T(8,128)S(1)} %get-tuple-element.13.new_w, ...), custom_call_target="tpu_custom_call" | custom-call | tf_op jit(solution)/shard_map/finish/pallas_call | solution.py:823
Async XLA Ops:
  0.6 139.6 %copy-start = (s32[8]{0:T(128)S(1)}, s32[8]{0:T(128)}, u32[]{:S(2)}) copy-start(s32[8]{0:T(128)} %owner_hbm.3) | copy-start | bytes 100

commit v5 on v4

--- a/solution.py
+++ b/solution.py
@@ -303,6 +303,8 @@
     def part(zs, pr, da, h):
         return g_all.at[zs, pr, h, (cx + da + NX) % NX]
 
+    pair_of = x_slot.at[0]
+
     def push(ref, zs, k, dd):
         send(ref, ref, ag_send, ag_recv.at[zs, k], z, dd)
 
@@ -448,17 +450,16 @@
                 zs = column(it)
                 landed(it)
                 push(whole(zs, duo, 0), zs, 0, right)
-                push(whole(zs, duo, 0), zs, 1, left)
+                push(whole(zs, duo, 0), zs, 0, left)
                 push(whole(zs, duo, 0), zs, 3, inner)
 
             @pl.when((it >= 1) & (it < NZ + 1))
             def _():
                 zs = column(it - 1)
-                arrived(whole(zs, duo, -1), ag_recv.at[zs, 0])
+                arrived(pair_of, ag_recv.at[zs, 0])
                 push(part(zs, duo, -1, 0), zs, 2, right)
+                push(part(zs, duo, 1, 1), zs, 2, left)
                 push(whole(zs, duo, -1), zs, 3, inner)
-                arrived(whole(zs, duo, 1), ag_recv.at[zs, 1])
-                push(part(zs, duo, 1, 1), zs, 2, left)
                 push(whole(zs, duo, 1), zs, 3, inner)
 
             feed(it)
@@ -486,17 +487,16 @@
                 landed(it)
                 push(whole(zs, duo, 0), zs, 3, inner)
                 push(whole(zs, duo, 0), zs, 0, right)
-                push(whole(zs, duo, 0), zs, 1, left)
+                push(whole(zs, duo, 0), zs, 0, left)
 
             @pl.when((it >= 1) & (it < NZ + 1))
             def _():
                 zs = column(it - 1)
                 arrived(whole(zs, 1 - duo, 0), ag_recv.at[zs, 3])
-                push(whole(zs, 1 - duo, 0), zs, 4, right)
-                push(whole(zs, 1 - duo, 0), zs, 5, left)
-                arrived(whole(zs, duo, -1), ag_recv.at[zs, 0])
+                push(whole(zs, 1 - duo, 0), zs, 1, right)
+                push(whole(zs, 1 - duo, 0), zs, 1, left)
+                arrived(pair_of, ag_recv.at[zs, 0])
                 push(part(zs, duo, -1, 0), zs, 2, right)
-                arrived(whole(zs, duo, 1), ag_recv.at[zs, 1])
                 push(part(zs, duo, 1, 1), zs, 2, left)
 
             feed(it)
@@ -504,16 +504,15 @@
             @pl.when((it >= 2) & (it < NZ + 2))
             def _():
                 zs = column(it - 2)
-                arrived(whole(zs, 1 - duo, -1), ag_recv.at[zs, 4])
-                push(part(zs, 1 - duo, -1, 0), zs, 6, right)
-                arrived(whole(zs, 1 - duo, 1), ag_recv.at[zs, 5])
-                push(part(zs, 1 - duo, 1, 1), zs, 6, left)
+                arrived(pair_of, ag_recv.at[zs, 1])
+                push(part(zs, 1 - duo, -1, 0), zs, 4, right)
+                push(part(zs, 1 - duo, 1, 1), zs, 4, left)
                 arrived(whole(zs, duo, 2), ag_recv.at[zs, 2])
 
             @pl.when((it >= 3) & (it < NZ + 3))
             def _():
                 zs = column(it - 3)
-                arrived(whole(zs, 1 - duo, 2), ag_recv.at[zs, 6])
+                arrived(whole(zs, 1 - duo, 2), ag_recv.at[zs, 4])
 
             x_stages(it)
     multiply(2 * NZ - 1, final=True)
@@ -579,13 +578,13 @@
             piece(s, k, r),
             piece(s, k, r),
             wz_send,
-            wz_recv.at[way, hop, 2 * k + r],
+            wz_recv.at[way, hop, k],
             (up, down)[way],
             d,
         )
 
-    def came(s, k, r, way, hop):
-        arrived(piece(s, k, r), wz_recv.at[way, hop, 2 * k + r])
+    def came(s, k, way, hop):
+        arrived(slabs.at[s, mates[k][0]], wz_recv.at[way, hop, k])
 
     def renew(k):
         for r in range(2):
@@ -607,11 +606,11 @@
 
     def onward(j, ks):
         for k in ks:
-            for r in range(2):
-                for way in range(2):
-                    if j < 3 or k % 2 == way:
-                        s = ((z + NZ - j) % NZ, (z + j) % NZ)[way]
-                        came(s, k, r, way, j - 1)
+            for way in range(2):
+                if j < 3 or k % 2 == way:
+                    s = ((z + NZ - j) % NZ, (z + j) % NZ)[way]
+                    came(s, k, way, j - 1)
+                    for r in range(2):
                         pass_on(s, k, r, way, j)
     renew(0)
     arrived(grad.at[:, columns(1)], half_recv.at[0])
@@ -673,9 +672,8 @@
         table[0, b] = jnp.where(hits > 0, moved, flat)
     for k in range(4):
         way = k % 2
-        for r in range(2):
-            came(((z + 3) % NZ, (z + NZ - 3) % NZ)[way], k, r, 1 - way, 2)
-            came(far, k, r, way, 3)
+        came(((z + 3) % NZ, (z + NZ - 3) % NZ)[way], k, 1 - way, 2)
+        came(far, k, way, 3)
     arrived(g_slot.at[0:6], gz_send)
     for k in range(3):
         arrived(g_slot.at[0, 0], go_send.at[k])
@@ -794,7 +792,7 @@
             dma,
             dma((NZ, 2)),
             dma,
-            dma((NZ, 7)),
+            dma((NZ, 5)),
             dma,
             dma((3,)),
             dma,
@@ -804,7 +802,7 @@
             dma,
             dma,
             dma,
-            dma((2, 4, 8)),
+            dma((2, 4, 4)),
         ],
         compiler_params=pltpu.CompilerParams(
             collective_id=0, has_side_effects=True, vmem_limit_bytes=60_160_000

time: 143 us -> 144 us (level)
  no operation moved by 1% of the time
where the time goes in v5:
time: 144 us; the launch traced here: 143 us
  Pallas kernels  143 us (99%)
    pallas_call x1, Pallas kernels, local(): pl.pallas_call(step_kernel, name='step', out_shape=(pltpu.VMEM((NZ, 4, ro...  140 us
    pallas_call x1, Pallas kernels, local(): pl.pallas_call(finish_kernel, name='finish', in_specs=[anywhere] * 5, out...  3.09 us

profile of v5, /device:TPU:1, one launch (start us, length us, event | category | flops | bytes accessed | tf_op | source)
XLA Modules:
  0.0 143.4 jit_solution(7348809574278493816)
XLA Ops:
  0.6 0.0 copy-start
  0.6 139.7 %step.1 = (bf16[8,4,128,512]{3,2,1,0:T(8,128)(2,1)S(1)}, f32[1,128,2048]{2,1,0:T(8,128)S(1)}, f32[1,128,2048]{2,1,0:T(8,128)S(1)}, f32[1,8,128,128]{3,2,1,0:T(8,128)S(1)}) custom-call(s32[8]{0:T(128)} %owner_hbm.3, s32[1,1,64]{2,1,0:T(1,128)} %ids_hbm.1, s32[1,1,32]{2,1,0:T(1,128)} %counts_hbm.1, bf16[8,1024,128]{2,1,0:T(8,128)(2,1)} %x_hbm.1, ...), custom_call_target="tpu_custom_call" | custom-call | tf_op jit(solution)/shard_map/step/pallas_call | solution.py:742
  140.3 0.0 copy-done
  140.3 3.1 %finish.1 = (bf16[8,128,2048]{2,1,0:T(8,128)(2,1)}, f32[1,128,2048]{2,1,0:T(8,128)}, f32[1,128,2048]{2,1,0:T(8,128)}, f32[1,8,128,128]{3,2,1,0:T(8,128)}) custom-call(s32[8]{0:T(128)S(1)} %copy-done, bf16[8,4,128,512]{3,2,1,0:T(8,128)(2,1)S(1)} %get-tuple-element.12.slots, f32[1,128,2048]{2,1,0:T(8,128)S(1)} %get-tuple-element.13.new_w, ...), custom_call_target="tpu_custom_call" | custom-call | tf_op jit(solution)/shard_map/finish/pallas_call | solution.py:821
Async XLA Ops:
  0.6 139.7 %copy-start = (s32[8]{0:T(128)S(1)}, s32[8]{0:T(128)}, u32[]{:S(2)}) copy-start(s32[8]{0:T(128)} %owner_hbm.3) | copy-start | bytes 100
